TPU v7x, 32 devices: a whole 2x2x4 slice. The times are simulated.
32 devices in a mesh: section: 8 (over z, y), dp: 4 (over x, core).
Axes of the slice: x: 2, y: 2, z: 4, core: 2. Of those that a mesh axis runs over, the one named last changes fastest.
Arguments:
- vit_weight: bfloat16 [8, 1280, 1280], P('section', 'dp'), may hold values from -0.078125 to 0.078125
- t5_weight: bfloat16 [8, 2048, 2048], P('section', 'dp'), may hold values from -0.0625 to 0.0625
- vit_saved: bfloat16 [8, 4, 128, 1280], P('section', None, 'dp'), may hold values from -6 to 6
- t5_saved: bfloat16 [8, 4, 128, 2048], P('section', None, 'dp'), may hold values from -6 to 6
- vit_top_grad: bfloat16 [4, 128, 1280], P(None, 'dp'), may hold values from -6 to 6
- t5_top_grad: bfloat16 [4, 128, 2048], P(None, 'dp'), may hold values from -6 to 6
Outputs:
- vit_input_grads: bfloat16 [8, 4, 128, 1280], P('section', None, 'dp')
- t5_input_grads: bfloat16 [8, 4, 128, 2048], P('section', None, 'dp')
- vit_weight_grads: float32 [8, 1280, 1280], P('section', 'dp')
- t5_weight_grads: float32 [8, 2048, 2048], P('section', 'dp')
All inputs are finite; a program needn't handle non-finite values.
Results may differ from a plain program's by a relative error of at most 0.02.
Values may be sent and summed in bfloat16 or wider, within the bound.
A program may use at most 128 MiB of HBM per device.

v0:
```python
import jax
import jax.numpy as jnp
from jax import lax
from jax.sharding import PartitionSpec as P

root_half = 0.7071067811865476
inv_root_tau = 0.3989422804014327


def shifted(block, axis, distance):
    devices = range(lax.axis_size(axis))
    route = [(i - distance, i) for i in devices if i - distance in devices]
    return lax.ppermute(block, axis, route)


def gelu_slope(preact):
    cumulative = 0.5 * (1.0 + lax.erf(preact * root_half))
    density = jnp.exp(-0.5 * preact * preact) * inv_root_tau
    return cumulative + preact * density


def layer_back(grad_above, saved_input, weight):
    preact = jnp.dot(saved_input, weight, preferred_element_type=jnp.float32)
    upper = grad_above.astype(jnp.float32)
    local_grad = (upper * gelu_slope(preact)).astype(jnp.bfloat16)
    through = lax.dot_general(
        local_grad, weight, (((1,), (1,)), ((), ())), preferred_element_type=jnp.float32
    )
    return ((upper + through).astype(jnp.bfloat16), local_grad)


def branch_tick(
    micro_index, received, top_grad, saved_all, weight, grad_buffer, local_buffer, is_last
):
    micro_count = saved_all.shape[0]
    active = jnp.logical_and(micro_index >= 0, micro_index < micro_count)
    micro_slot = jnp.clip(micro_index, 0, micro_count - 1)
    from_joining = lax.dynamic_index_in_dim(top_grad, micro_slot, 0, keepdims=False)
    incoming = jnp.where(is_last, from_joining, received)
    saved_input = lax.dynamic_index_in_dim(saved_all, micro_slot, 0, keepdims=False)

    def advance(operands):
        grad_above, layer_input, grads_now, locals_now = operands
        grad_below, local_grad = layer_back(grad_above, layer_input, weight)
        grads_now = lax.dynamic_update_index_in_dim(grads_now, grad_below, micro_slot, 0)
        locals_now = lax.dynamic_update_index_in_dim(locals_now, local_grad, micro_slot, 0)
        return (grad_below, grads_now, locals_now)

    def passed(operands):
        return (jnp.zeros_like(operands[0]), operands[2], operands[3])

    return lax.cond(active, advance, passed, (incoming, saved_input, grad_buffer, local_buffer))


def vit_weight_total(inputs, locals_all, token_scale):
    input_flat = inputs.reshape(-1, inputs.shape[2])
    local_flat = locals_all.reshape(-1, inputs.shape[2])
    return lax.psum_scatter(
        (
            lax.dot_general(
                input_flat, local_flat, (((0,), (0,)), ((), ())), preferred_element_type=jnp.float32
            )
            * token_scale
        ).astype(jnp.bfloat16),
        "dp",
        scatter_dimension=0,
        tiled=True,
    ).astype(jnp.float32)


def t5_weight_total(inputs, locals_all, token_scale):
    input_flat = inputs.reshape(-1, inputs.shape[2])
    local_flat = locals_all.reshape(-1, inputs.shape[2])
    return lax.psum_scatter(
        (
            lax.dot_general(
                input_flat, local_flat, (((0,), (0,)), ((), ())), preferred_element_type=jnp.float32
            )
            * token_scale
        ).astype(jnp.bfloat16),
        "dp",
        scatter_dimension=0,
        tiled=True,
    ).astype(jnp.float32)


def shards(vit_weight, t5_weight, vit_saved, t5_saved, vit_top_grad, t5_top_grad):
    section_count = lax.axis_size("section")
    section_index = lax.axis_index("section")
    is_last = section_index == section_count - 1
    vit_full, t5_full = (
        lax.all_gather(vit_weight[0], "dp", axis=0, tiled=True),
        lax.all_gather(t5_weight[0], "dp", axis=0, tiled=True),
    )
    vit_shape = vit_saved.shape[1:]
    token_scale = 1.0 / (vit_shape[0] * vit_shape[1])
    vit_inputs = vit_saved[0]
    t5_inputs = t5_saved[0]
    micro_count = vit_inputs.shape[0]
    depth = section_count - 1 - section_index
    vit_start = (
        jnp.zeros_like(vit_top_grad[0]),
        jnp.zeros_like(vit_inputs),
        jnp.zeros_like(vit_inputs),
    )
    t5_start = (
        jnp.zeros_like(t5_top_grad[0]),
        jnp.zeros_like(t5_inputs),
        jnp.zeros_like(t5_inputs),
    )

    def text_tick(tick_index, state_tuple):
        t5_recv, t5_grads, t5_locals = state_tuple
        t5_below, t5_grads, t5_locals = branch_tick(
            tick_index - depth,
            t5_recv,
            t5_top_grad,
            t5_inputs,
            t5_full,
            t5_grads,
            t5_locals,
            is_last,
        )
        t5_recv = shifted(t5_below, "section", -1)
        return (t5_recv, t5_grads, t5_locals)

    def image_tick(tick_index, state_tuple):
        vit_recv, vit_grads, vit_locals = state_tuple
        vit_below, vit_grads, vit_locals = branch_tick(
            tick_index - depth,
            vit_recv,
            vit_top_grad,
            vit_inputs,
            vit_full,
            vit_grads,
            vit_locals,
            is_last,
        )
        vit_recv = shifted(vit_below, "section", -1)
        return (vit_recv, vit_grads, vit_locals)

    text_state = lax.fori_loop(0, section_count + micro_count - 1, text_tick, t5_start)
    t5_grads, t5_locals = (text_state[1], text_state[2])
    t5_sum = t5_weight_total(t5_inputs, t5_locals, token_scale)
    image_state = lax.fori_loop(0, section_count + micro_count - 1, image_tick, vit_start)
    vit_grads, vit_locals = (image_state[1], image_state[2])
    vit_sum = vit_weight_total(vit_inputs, vit_locals, token_scale)
    return (vit_grads[None], t5_grads[None], vit_sum[None], t5_sum[None])


def solution(mesh):
    placed = (
        P("section", "dp", None),
        P("section", "dp", None),
        P("section", None, "dp", None),
        P("section", None, "dp", None),
        P(None, "dp", None),
        P(None, "dp", None),
    )
    return jax.shard_map(
        shards,
        mesh=mesh,
        in_specs=placed,
        out_specs=(
            P("section", None, "dp", None),
            P("section", None, "dp", None),
            P("section", "dp", None),
            P("section", "dp", None),
        ),
        check_vma=False,
    )
```

profile of v0, /device:TPU:0, one launch (start us, length us, event | category | flops | bytes accessed | tf_op | source)
XLA Modules:
  0.0 422.4 jit_solution(1708523490718756417)
XLA Ops:
  8.7 32.8 %all-gather.5.cloned.1.call-done = bf16[1,1280,1280]{2,1,0:T(8,128)(2,1)} async-done(((bf16[1,320,1280]{2,1,0:T(8,128)(2,1)}), bf16[1,1280,1280]{2,1,0:T(8,128)(2,1)}) %all-gather.5.cloned.1.call-update) | async-done | bytes 3276816 | tf_op jit(solution)/shard_map/all_gather | solution.py:92
  43.0 136.0 %while.34 = (s32[]{:T(128)}, bf16[32,1280]{1,0:T(8,128)(2,1)S(1)}, bf16[4,32,1280]{2,1,0:T(8,128)(2,1)}, bf16[4,32,1280]{2,1,0:T(8,128)(2,1)}, s32[]{:T(128)}, /...) while((s32[]{:T(128)}, bf16[32,1280]{1,0:T(8,128)(2,1)S(1)}, ...), condition=%wide.region_3.4_spmd, body=%wide.region_0.3_spmd.sunk | while | flops 210862080 | bytes 21139296 | solution.py:145
  57.6 5.9 %collective-permute-done = bf16[32,1280]{1,0:T(8,128)(2,1)S(1)} collective-permute-done((bf16[32,1280]{1,0:T(8,128)(2,1)S(1)}, bf16[32,1280]{1,0:T(8,128)(2,1)S(1)}, u32[]{:S(2)}, u32[]{:S(2)}) %collective-permute-start) | collective-permute-done | bytes 81952 | tf_op jit(solution)/shard_map/while/body/eval_jaxpr/ppermute | solution.py:13
  64.9 5.9 %collective-permute-done = bf16[32,1280]{1,0:T(8,128)(2,1)S(1)} collective-permute-done((bf16[32,1280]{1,0:T(8,128)(2,1)S(1)}, bf16[32,1280]{1,0:T(8,128)(2,1)S(1)}, u32[]{:S(2)}, u32[]{:S(2)}) %collective-permute-start) | collective-permute-done | bytes 81952 | tf_op jit(solution)/shard_map/while/body/eval_jaxpr/ppermute | solution.py:13
  72.1 5.9 %collective-permute-done = bf16[32,1280]{1,0:T(8,128)(2,1)S(1)} collective-permute-done((bf16[32,1280]{1,0:T(8,128)(2,1)S(1)}, bf16[32,1280]{1,0:T(8,128)(2,1)S(1)}, u32[]{:S(2)}, u32[]{:S(2)}) %collective-permute-start) | collective-permute-done | bytes 81952 | tf_op jit(solution)/shard_map/while/body/eval_jaxpr/ppermute | solution.py:13
  79.4 5.9 %collective-permute-done = bf16[32,1280]{1,0:T(8,128)(2,1)S(1)} collective-permute-done((bf16[32,1280]{1,0:T(8,128)(2,1)S(1)}, bf16[32,1280]{1,0:T(8,128)(2,1)S(1)}, u32[]{:S(2)}, u32[]{:S(2)}) %collective-permute-start) | collective-permute-done | bytes 81952 | tf_op jit(solution)/shard_map/while/body/eval_jaxpr/ppermute | solution.py:13
  86.7 39.9 %collective-permute-done = bf16[32,1280]{1,0:T(8,128)(2,1)S(1)} collective-permute-done((bf16[32,1280]{1,0:T(8,128)(2,1)S(1)}, bf16[32,1280]{1,0:T(8,128)(2,1)S(1)}, u32[]{:S(2)}, u32[]{:S(2)}) %collective-permute-start) | collective-permute-done | bytes 81952 | tf_op jit(solution)/shard_map/while/body/eval_jaxpr/ppermute | solution.py:13
  126.5 6.1 %conditional.4 = (bf16[32,1280]{1,0:T(8,128)(2,1)S(1)}, bf16[4,32,1280]{2,1,0:T(8,128)(2,1)}, bf16[4,32,1280]{2,1,0:T(8,128)(2,1)}) conditional(s32[]{:T(128)} %convert_element_type.116, (bf16[4,32,1280]{2,1,0:T(8,128)(2,1)}, bf16[4,32,1280]{2,1,0:T(8,128)(2,1)}) %tuple.96, (pred[]{:T(512)}, s32[]{:T(128)}, bf16[4,32,1280]{2,1,0:T(8,128)(2,1)}, ...), branch_computations={%region_1.1_spmd, %region_2.2_spmd} | conditional | flops 210862080 | bytes 20811340 | solution.py:52
  133.9 5.9 %collective-permute-done = bf16[32,1280]{1,0:T(8,128)(2,1)S(1)} collective-permute-done((bf16[32,1280]{1,0:T(8,128)(2,1)S(1)}, bf16[32,1280]{1,0:T(8,128)(2,1)S(1)}, u32[]{:S(2)}, u32[]{:S(2)}) %collective-permute-start) | collective-permute-done | bytes 81952 | tf_op jit(solution)/shard_map/while/body/eval_jaxpr/ppermute | solution.py:13
  139.9 6.1 %conditional.4 = (bf16[32,1280]{1,0:T(8,128)(2,1)S(1)}, bf16[4,32,1280]{2,1,0:T(8,128)(2,1)}, bf16[4,32,1280]{2,1,0:T(8,128)(2,1)}) conditional(s32[]{:T(128)} %convert_element_type.116, (bf16[4,32,1280]{2,1,0:T(8,128)(2,1)}, bf16[4,32,1280]{2,1,0:T(8,128)(2,1)}) %tuple.96, (pred[]{:T(512)}, s32[]{:T(128)}, bf16[4,32,1280]{2,1,0:T(8,128)(2,1)}, ...), branch_computations={%region_1.1_spmd, %region_2.2_spmd} | conditional | flops 210862080 | bytes 20811340 | solution.py:52
  147.3 6.0 %collective-permute-done = bf16[32,1280]{1,0:T(8,128)(2,1)S(1)} collective-permute-done((bf16[32,1280]{1,0:T(8,128)(2,1)S(1)}, bf16[32,1280]{1,0:T(8,128)(2,1)S(1)}, u32[]{:S(2)}, u32[]{:S(2)}) %collective-permute-start) | collective-permute-done | bytes 81952 | tf_op jit(solution)/shard_map/while/body/eval_jaxpr/ppermute | solution.py:13
  153.3 6.1 %conditional.4 = (bf16[32,1280]{1,0:T(8,128)(2,1)S(1)}, bf16[4,32,1280]{2,1,0:T(8,128)(2,1)}, bf16[4,32,1280]{2,1,0:T(8,128)(2,1)}) conditional(s32[]{:T(128)} %convert_element_type.116, (bf16[4,32,1280]{2,1,0:T(8,128)(2,1)}, bf16[4,32,1280]{2,1,0:T(8,128)(2,1)}) %tuple.96, (pred[]{:T(512)}, s32[]{:T(128)}, bf16[4,32,1280]{2,1,0:T(8,128)(2,1)}, ...), branch_computations={%region_1.1_spmd, %region_2.2_spmd} | conditional | flops 210862080 | bytes 20811340 | solution.py:52
  160.7 5.9 %collective-permute-done = bf16[32,1280]{1,0:T(8,128)(2,1)S(1)} collective-permute-done((bf16[32,1280]{1,0:T(8,128)(2,1)S(1)}, bf16[32,1280]{1,0:T(8,128)(2,1)S(1)}, u32[]{:S(2)}, u32[]{:S(2)}) %collective-permute-start) | collective-permute-done | bytes 81952 | tf_op jit(solution)/shard_map/while/body/eval_jaxpr/ppermute | solution.py:13
  166.6 6.1 %conditional.4 = (bf16[32,1280]{1,0:T(8,128)(2,1)S(1)}, bf16[4,32,1280]{2,1,0:T(8,128)(2,1)}, bf16[4,32,1280]{2,1,0:T(8,128)(2,1)}) conditional(s32[]{:T(128)} %convert_element_type.116, (bf16[4,32,1280]{2,1,0:T(8,128)(2,1)}, bf16[4,32,1280]{2,1,0:T(8,128)(2,1)}) %tuple.96, (pred[]{:T(512)}, s32[]{:T(128)}, bf16[4,32,1280]{2,1,0:T(8,128)(2,1)}, ...), branch_computations={%region_1.1_spmd, %region_2.2_spmd} | conditional | flops 210862080 | bytes 20811340 | solution.py:52
  185.8 146.2 %while.35 = (s32[]{:T(128)}, bf16[32,2048]{1,0:T(8,128)(2,1)S(1)}, bf16[4,32,2048]{2,1,0:T(8,128)(2,1)S(1)}, bf16[4,32,2048]{2,1,0:T(8,128)(2,1)S(1)}, s32[]{:T(...) while((s32[]{:T(128)}, bf16[32,2048]{1,0:T(8,128)(2,1)S(1)}, ...), condition=%wide.region_7.8_spmd, body=%wide.region_4.7_spmd.sunk | while | flops 538705920 | bytes 52694368 | solution.py:142
  187.1 5.6 %collective-permute-done.1 = bf16[32,2048]{1,0:T(8,128)(2,1)S(1)} collective-permute-done((bf16[32,2048]{1,0:T(8,128)(2,1)S(1)}, bf16[32,2048]{1,0:T(8,128)(2,1)S(1)}, u32[]{:S(2)}, u32[]{:S(2)}) %collective-permute-start.1) | collective-permute-done | bytes 131104 | tf_op jit(solution)/shard_map/while/body/eval_jaxpr/ppermute | solution.py:13
  194.1 5.9 %collective-permute-done.1 = bf16[32,2048]{1,0:T(8,128)(2,1)S(1)} collective-permute-done((bf16[32,2048]{1,0:T(8,128)(2,1)S(1)}, bf16[32,2048]{1,0:T(8,128)(2,1)S(1)}, u32[]{:S(2)}, u32[]{:S(2)}) %collective-permute-start.1) | collective-permute-done | bytes 131104 | tf_op jit(solution)/shard_map/while/body/eval_jaxpr/ppermute | solution.py:13
  201.3 6.6 %collective-permute-done.1 = bf16[32,2048]{1,0:T(8,128)(2,1)S(1)} collective-permute-done((bf16[32,2048]{1,0:T(8,128)(2,1)S(1)}, bf16[32,2048]{1,0:T(8,128)(2,1)S(1)}, u32[]{:S(2)}, u32[]{:S(2)}) %collective-permute-start.1) | collective-permute-done | bytes 131104 | tf_op jit(solution)/shard_map/while/body/eval_jaxpr/ppermute | solution.py:13
  209.2 6.6 %collective-permute-done.1 = bf16[32,2048]{1,0:T(8,128)(2,1)S(1)} collective-permute-done((bf16[32,2048]{1,0:T(8,128)(2,1)S(1)}, bf16[32,2048]{1,0:T(8,128)(2,1)S(1)}, u32[]{:S(2)}, u32[]{:S(2)}) %collective-permute-start.1) | collective-permute-done | bytes 131104 | tf_op jit(solution)/shard_map/while/body/eval_jaxpr/ppermute | solution.py:13
  217.2 5.6 %collective-permute-done.1 = bf16[32,2048]{1,0:T(8,128)(2,1)S(1)} collective-permute-done((bf16[32,2048]{1,0:T(8,128)(2,1)S(1)}, bf16[32,2048]{1,0:T(8,128)(2,1)S(1)}, u32[]{:S(2)}, u32[]{:S(2)}) %collective-permute-start.1) | collective-permute-done | bytes 131104 | tf_op jit(solution)/shard_map/while/body/eval_jaxpr/ppermute | solution.py:13
  224.1 5.6 %collective-permute-done.1 = bf16[32,2048]{1,0:T(8,128)(2,1)S(1)} collective-permute-done((bf16[32,2048]{1,0:T(8,128)(2,1)S(1)}, bf16[32,2048]{1,0:T(8,128)(2,1)S(1)}, u32[]{:S(2)}, u32[]{:S(2)}) %collective-permute-start.1) | collective-permute-done | bytes 131104 | tf_op jit(solution)/shard_map/while/body/eval_jaxpr/ppermute | solution.py:13
  231.0 35.7 %collective-permute-done.1 = bf16[32,2048]{1,0:T(8,128)(2,1)S(1)} collective-permute-done((bf16[32,2048]{1,0:T(8,128)(2,1)S(1)}, bf16[32,2048]{1,0:T(8,128)(2,1)S(1)}, u32[]{:S(2)}, u32[]{:S(2)}) %collective-permute-start.1) | collective-permute-done | bytes 131104 | tf_op jit(solution)/shard_map/while/body/eval_jaxpr/ppermute | solution.py:13
  266.6 8.3 %conditional.5 = (bf16[32,2048]{1,0:T(8,128)(2,1)S(1)}, bf16[4,32,2048]{2,1,0:T(8,128)(2,1)S(1)}, bf16[4,32,2048]{2,1,0:T(8,128)(2,1)S(1)}) conditional(s32[]{:T(128)} %convert_element_type.117, (bf16[4,32,2048]{2,1,0:T(8,128)(2,1)S(1)}, bf16[4,32,2048]{2,1,0:T(8,128)(2,1)S(1)}) %tuple.99, (pred[]{:T(512)}, s32[]{:T(128)}, ...), branch_computations={%region_5.5_spmd, %region_6.6_spmd} | conditional | flops 538705920 | bytes 52169804 | solution.py:52
  276.3 7.8 %collective-permute-done.1 = bf16[32,2048]{1,0:T(8,128)(2,1)S(1)} collective-permute-done((bf16[32,2048]{1,0:T(8,128)(2,1)S(1)}, bf16[32,2048]{1,0:T(8,128)(2,1)S(1)}, u32[]{:S(2)}, u32[]{:S(2)}) %collective-permute-start.1) | collective-permute-done | bytes 131104 | tf_op jit(solution)/shard_map/while/body/eval_jaxpr/ppermute | solution.py:13
  284.1 8.4 %conditional.5 = (bf16[32,2048]{1,0:T(8,128)(2,1)S(1)}, bf16[4,32,2048]{2,1,0:T(8,128)(2,1)S(1)}, bf16[4,32,2048]{2,1,0:T(8,128)(2,1)S(1)}) conditional(s32[]{:T(128)} %convert_element_type.117, (bf16[4,32,2048]{2,1,0:T(8,128)(2,1)S(1)}, bf16[4,32,2048]{2,1,0:T(8,128)(2,1)S(1)}) %tuple.99, (pred[]{:T(512)}, s32[]{:T(128)}, ...), branch_computations={%region_5.5_spmd, %region_6.6_spmd} | conditional | flops 538705920 | bytes 52169804 | solution.py:52
  293.8 7.2 %collective-permute-done.1 = bf16[32,2048]{1,0:T(8,128)(2,1)S(1)} collective-permute-done((bf16[32,2048]{1,0:T(8,128)(2,1)S(1)}, bf16[32,2048]{1,0:T(8,128)(2,1)S(1)}, u32[]{:S(2)}, u32[]{:S(2)}) %collective-permute-start.1) | collective-permute-done | bytes 131104 | tf_op jit(solution)/shard_map/while/body/eval_jaxpr/ppermute | solution.py:13
  300.9 8.3 %conditional.5 = (bf16[32,2048]{1,0:T(8,128)(2,1)S(1)}, bf16[4,32,2048]{2,1,0:T(8,128)(2,1)S(1)}, bf16[4,32,2048]{2,1,0:T(8,128)(2,1)S(1)}) conditional(s32[]{:T(128)} %convert_element_type.117, (bf16[4,32,2048]{2,1,0:T(8,128)(2,1)S(1)}, bf16[4,32,2048]{2,1,0:T(8,128)(2,1)S(1)}) %tuple.99, (pred[]{:T(512)}, s32[]{:T(128)}, ...), branch_computations={%region_5.5_spmd, %region_6.6_spmd} | conditional | flops 538705920 | bytes 52169804 | solution.py:52
  310.6 6.2 %collective-permute-done.1 = bf16[32,2048]{1,0:T(8,128)(2,1)S(1)} collective-permute-done((bf16[32,2048]{1,0:T(8,128)(2,1)S(1)}, bf16[32,2048]{1,0:T(8,128)(2,1)S(1)}, u32[]{:S(2)}, u32[]{:S(2)}) %collective-permute-start.1) | collective-permute-done | bytes 131104 | tf_op jit(solution)/shard_map/while/body/eval_jaxpr/ppermute | solution.py:13
  316.8 8.3 %conditional.5 = (bf16[32,2048]{1,0:T(8,128)(2,1)S(1)}, bf16[4,32,2048]{2,1,0:T(8,128)(2,1)S(1)}, bf16[4,32,2048]{2,1,0:T(8,128)(2,1)S(1)}) conditional(s32[]{:T(128)} %convert_element_type.117, (bf16[4,32,2048]{2,1,0:T(8,128)(2,1)S(1)}, bf16[4,32,2048]{2,1,0:T(8,128)(2,1)S(1)}) %tuple.99, (pred[]{:T(512)}, s32[]{:T(128)}, ...), branch_computations={%region_5.5_spmd, %region_6.6_spmd} | conditional | flops 538705920 | bytes 52169804 | solution.py:52
  326.4 5.6 %collective-permute-done.1 = bf16[32,2048]{1,0:T(8,128)(2,1)S(1)} collective-permute-done((bf16[32,2048]{1,0:T(8,128)(2,1)S(1)}, bf16[32,2048]{1,0:T(8,128)(2,1)S(1)}, u32[]{:S(2)}, u32[]{:S(2)}) %collective-permute-start.1) | collective-permute-done | bytes 131104 | tf_op jit(solution)/shard_map/while/body/eval_jaxpr/ppermute | solution.py:13
  332.0 5.6 %fusion.50 = bf16[2048,2048]{0,1:T(8,128)(2,1)} fusion(bf16[128,2048]{1,0:T(8,128)(2,1)S(1)} %bitcast.77, bf16[128,2048]{1,0:T(8,128)(2,1)S(1)} %bitcast.79), kind=kOutput, calls=%fused_computation.60 | convolution fusion | flops 1082130432 | bytes 9437184 | tf_op jit(solution)/shard_map/dot_general | solution.py:76
  341.1 65.3 %reduce-scatter.5.cloned.1.call-done = bf16[512,2048]{0,1:T(8,128)(2,1)} async-done(((bf16[2048,2048]{0,1:T(8,128)(2,1)}), bf16[512,2048]{0,1:T(8,128)(2,1)}) %reduce-scatter.5.cloned.1.call-update) | async-done | bytes 2097168 | tf_op jit(solution)/shard_map/reduce_scatter | solution.py:74
  (114 shorter events, 124.8 us)
Async XLA Ops:
  7.2 34.4 %all-gather.5.cloned.1.call-start = ((), (), s32[]{:S(2)}) async-start(), calls=%async_computation.3 | async-start | bytes 4096000 | tf_op jit(solution)/shard_map/all_gather | solution.py:92
  7.9 176.8 %all-gather.7.cloned.1.call-start = ((), (), s32[]{:S(2)}) async-start(), calls=%async_computation.4 | async-start | bytes 10485760 | tf_op jit(solution)/shard_map/all_gather | solution.py:93
  8.6 329.0 %reduce-scatter.7.cloned.1.call-start = ((), (), s32[]{:S(2)}) async-start(), calls=%async_computation.5 | async-start | bytes 4096000
  43.1 6.5 %collective-permute-start = (bf16[32,1280]{1,0:T(8,128)(2,1)S(1)}, bf16[32,1280]{1,0:T(8,128)(2,1)S(1)}, u32[]{:S(2)}, u32[]{:S(2)}) collective-permute-start(bf16[32,1280]{1,0:T(8,128)(2,1)S(1)} %get-tuple-element.689), channel_id=1, source_target_pairs={{4,0},{8,4},{12,8},{16,12},{20,16},{24,20},{28,24},{5,1},{9,5},{13... | collective-permute-start | bytes 245768 | tf_op jit(solution)/shard_map/while/body/eval_jaxpr/ppermute | solution.py:13
  49.6 6.7 %collective-permute-start = (bf16[32,1280]{1,0:T(8,128)(2,1)S(1)}, bf16[32,1280]{1,0:T(8,128)(2,1)S(1)}, u32[]{:S(2)}, u32[]{:S(2)}) collective-permute-start(bf16[32,1280]{1,0:T(8,128)(2,1)S(1)} %get-tuple-element.689), channel_id=1, source_target_pairs={{4,0},{8,4},{12,8},{16,12},{20,16},{24,20},{28,24},{5,1},{9,5},{13... | collective-permute-start | bytes 245768 | tf_op jit(solution)/shard_map/while/body/eval_jaxpr/ppermute | solution.py:13
  56.3 7.2 %collective-permute-start = (bf16[32,1280]{1,0:T(8,128)(2,1)S(1)}, bf16[32,1280]{1,0:T(8,128)(2,1)S(1)}, u32[]{:S(2)}, u32[]{:S(2)}) collective-permute-start(bf16[32,1280]{1,0:T(8,128)(2,1)S(1)} %get-tuple-element.689), channel_id=1, source_target_pairs={{4,0},{8,4},{12,8},{16,12},{20,16},{24,20},{28,24},{5,1},{9,5},{13... | collective-permute-start | bytes 245768 | tf_op jit(solution)/shard_map/while/body/eval_jaxpr/ppermute | solution.py:13
  63.6 7.2 %collective-permute-start = (bf16[32,1280]{1,0:T(8,128)(2,1)S(1)}, bf16[32,1280]{1,0:T(8,128)(2,1)S(1)}, u32[]{:S(2)}, u32[]{:S(2)}) collective-permute-start(bf16[32,1280]{1,0:T(8,128)(2,1)S(1)} %get-tuple-element.689), channel_id=1, source_target_pairs={{4,0},{8,4},{12,8},{16,12},{20,16},{24,20},{28,24},{5,1},{9,5},{13... | collective-permute-start | bytes 245768 | tf_op jit(solution)/shard_map/while/body/eval_jaxpr/ppermute | solution.py:13
  70.8 7.2 %collective-permute-start = (bf16[32,1280]{1,0:T(8,128)(2,1)S(1)}, bf16[32,1280]{1,0:T(8,128)(2,1)S(1)}, u32[]{:S(2)}, u32[]{:S(2)}) collective-permute-start(bf16[32,1280]{1,0:T(8,128)(2,1)S(1)} %get-tuple-element.689), channel_id=1, source_target_pairs={{4,0},{8,4},{12,8},{16,12},{20,16},{24,20},{28,24},{5,1},{9,5},{13... | collective-permute-start | bytes 245768 | tf_op jit(solution)/shard_map/while/body/eval_jaxpr/ppermute | solution.py:13
  78.1 7.2 %collective-permute-start = (bf16[32,1280]{1,0:T(8,128)(2,1)S(1)}, bf16[32,1280]{1,0:T(8,128)(2,1)S(1)}, u32[]{:S(2)}, u32[]{:S(2)}) collective-permute-start(bf16[32,1280]{1,0:T(8,128)(2,1)S(1)} %get-tuple-element.689), channel_id=1, source_target_pairs={{4,0},{8,4},{12,8},{16,12},{20,16},{24,20},{28,24},{5,1},{9,5},{13... | collective-permute-start | bytes 245768 | tf_op jit(solution)/shard_map/while/body/eval_jaxpr/ppermute | solution.py:13
  85.4 41.2 %collective-permute-start = (bf16[32,1280]{1,0:T(8,128)(2,1)S(1)}, bf16[32,1280]{1,0:T(8,128)(2,1)S(1)}, u32[]{:S(2)}, u32[]{:S(2)}) collective-permute-start(bf16[32,1280]{1,0:T(8,128)(2,1)S(1)} %get-tuple-element.689), channel_id=1, source_target_pairs={{4,0},{8,4},{12,8},{16,12},{20,16},{24,20},{28,24},{5,1},{9,5},{13... | collective-permute-start | bytes 245768 | tf_op jit(solution)/shard_map/while/body/eval_jaxpr/ppermute | solution.py:13
  126.5 3.4 copy-start.1
  132.7 7.2 %collective-permute-start = (bf16[32,1280]{1,0:T(8,128)(2,1)S(1)}, bf16[32,1280]{1,0:T(8,128)(2,1)S(1)}, u32[]{:S(2)}, u32[]{:S(2)}) collective-permute-start(bf16[32,1280]{1,0:T(8,128)(2,1)S(1)} %get-tuple-element.689), channel_id=1, source_target_pairs={{4,0},{8,4},{12,8},{16,12},{20,16},{24,20},{28,24},{5,1},{9,5},{13... | collective-permute-start | bytes 245768 | tf_op jit(solution)/shard_map/while/body/eval_jaxpr/ppermute | solution.py:13
  146.0 7.3 %collective-permute-start = (bf16[32,1280]{1,0:T(8,128)(2,1)S(1)}, bf16[32,1280]{1,0:T(8,128)(2,1)S(1)}, u32[]{:S(2)}, u32[]{:S(2)}) collective-permute-start(bf16[32,1280]{1,0:T(8,128)(2,1)S(1)} %get-tuple-element.689), channel_id=1, source_target_pairs={{4,0},{8,4},{12,8},{16,12},{20,16},{24,20},{28,24},{5,1},{9,5},{13... | collective-permute-start | bytes 245768 | tf_op jit(solution)/shard_map/while/body/eval_jaxpr/ppermute | solution.py:13
  159.4 7.2 %collective-permute-start = (bf16[32,1280]{1,0:T(8,128)(2,1)S(1)}, bf16[32,1280]{1,0:T(8,128)(2,1)S(1)}, u32[]{:S(2)}, u32[]{:S(2)}) collective-permute-start(bf16[32,1280]{1,0:T(8,128)(2,1)S(1)} %get-tuple-element.689), channel_id=1, source_target_pairs={{4,0},{8,4},{12,8},{16,12},{20,16},{24,20},{28,24},{5,1},{9,5},{13... | collective-permute-start | bytes 245768 | tf_op jit(solution)/shard_map/while/body/eval_jaxpr/ppermute | solution.py:13
  172.7 6.3 %collective-permute-start = (bf16[32,1280]{1,0:T(8,128)(2,1)S(1)}, bf16[32,1280]{1,0:T(8,128)(2,1)S(1)}, u32[]{:S(2)}, u32[]{:S(2)}) collective-permute-start(bf16[32,1280]{1,0:T(8,128)(2,1)S(1)} %get-tuple-element.689), channel_id=1, source_target_pairs={{4,0},{8,4},{12,8},{16,12},{20,16},{24,20},{28,24},{5,1},{9,5},{13... | collective-permute-start | bytes 245768 | tf_op jit(solution)/shard_map/while/body/eval_jaxpr/ppermute | solution.py:13
  184.6 221.8 %reduce-scatter.5.cloned.1.call-start = ((), (), s32[]{:S(2)}) async-start(), calls=%async_computation.2 | async-start | bytes 10485760 | tf_op jit(solution)/shard_map/reduce_scatter | solution.py:74
  185.8 6.9 %collective-permute-start.1 = (bf16[32,2048]{1,0:T(8,128)(2,1)S(1)}, bf16[32,2048]{1,0:T(8,128)(2,1)S(1)}, u32[]{:S(2)}, u32[]{:S(2)}) collective-permute-start(bf16[32,2048]{1,0:T(8,128)(2,1)S(1)} %get-tuple-element.701), channel_id=1, source_target_pairs={{4,0},{8,4},{12,8},{16,12},{20,16},{24,20},{28,24},{5,1},{9,5},{13... | collective-permute-start | bytes 393224 | tf_op jit(solution)/shard_map/while/body/eval_jaxpr/ppermute | solution.py:13
  192.8 7.2 %collective-permute-start.1 = (bf16[32,2048]{1,0:T(8,128)(2,1)S(1)}, bf16[32,2048]{1,0:T(8,128)(2,1)S(1)}, u32[]{:S(2)}, u32[]{:S(2)}) collective-permute-start(bf16[32,2048]{1,0:T(8,128)(2,1)S(1)} %get-tuple-element.701), channel_id=1, source_target_pairs={{4,0},{8,4},{12,8},{16,12},{20,16},{24,20},{28,24},{5,1},{9,5},{13... | collective-permute-start | bytes 393224 | tf_op jit(solution)/shard_map/while/body/eval_jaxpr/ppermute | solution.py:13
  200.0 7.9 %collective-permute-start.1 = (bf16[32,2048]{1,0:T(8,128)(2,1)S(1)}, bf16[32,2048]{1,0:T(8,128)(2,1)S(1)}, u32[]{:S(2)}, u32[]{:S(2)}) collective-permute-start(bf16[32,2048]{1,0:T(8,128)(2,1)S(1)} %get-tuple-element.701), channel_id=1, source_target_pairs={{4,0},{8,4},{12,8},{16,12},{20,16},{24,20},{28,24},{5,1},{9,5},{13... | collective-permute-start | bytes 393224 | tf_op jit(solution)/shard_map/while/body/eval_jaxpr/ppermute | solution.py:13
  207.9 7.9 %collective-permute-start.1 = (bf16[32,2048]{1,0:T(8,128)(2,1)S(1)}, bf16[32,2048]{1,0:T(8,128)(2,1)S(1)}, u32[]{:S(2)}, u32[]{:S(2)}) collective-permute-start(bf16[32,2048]{1,0:T(8,128)(2,1)S(1)} %get-tuple-element.701), channel_id=1, source_target_pairs={{4,0},{8,4},{12,8},{16,12},{20,16},{24,20},{28,24},{5,1},{9,5},{13... | collective-permute-start | bytes 393224 | tf_op jit(solution)/shard_map/while/body/eval_jaxpr/ppermute | solution.py:13
  215.9 6.9 %collective-permute-start.1 = (bf16[32,2048]{1,0:T(8,128)(2,1)S(1)}, bf16[32,2048]{1,0:T(8,128)(2,1)S(1)}, u32[]{:S(2)}, u32[]{:S(2)}) collective-permute-start(bf16[32,2048]{1,0:T(8,128)(2,1)S(1)} %get-tuple-element.701), channel_id=1, source_target_pairs={{4,0},{8,4},{12,8},{16,12},{20,16},{24,20},{28,24},{5,1},{9,5},{13... | collective-permute-start | bytes 393224 | tf_op jit(solution)/shard_map/while/body/eval_jaxpr/ppermute | solution.py:13
  222.8 6.9 %collective-permute-start.1 = (bf16[32,2048]{1,0:T(8,128)(2,1)S(1)}, bf16[32,2048]{1,0:T(8,128)(2,1)S(1)}, u32[]{:S(2)}, u32[]{:S(2)}) collective-permute-start(bf16[32,2048]{1,0:T(8,128)(2,1)S(1)} %get-tuple-element.701), channel_id=1, source_target_pairs={{4,0},{8,4},{12,8},{16,12},{20,16},{24,20},{28,24},{5,1},{9,5},{13... | collective-permute-start | bytes 393224 | tf_op jit(solution)/shard_map/while/body/eval_jaxpr/ppermute | solution.py:13
  229.6 37.0 %collective-permute-start.1 = (bf16[32,2048]{1,0:T(8,128)(2,1)S(1)}, bf16[32,2048]{1,0:T(8,128)(2,1)S(1)}, u32[]{:S(2)}, u32[]{:S(2)}) collective-permute-start(bf16[32,2048]{1,0:T(8,128)(2,1)S(1)} %get-tuple-element.701), channel_id=1, source_target_pairs={{4,0},{8,4},{12,8},{16,12},{20,16},{24,20},{28,24},{5,1},{9,5},{13... | collective-permute-start | bytes 393224 | tf_op jit(solution)/shard_map/while/body/eval_jaxpr/ppermute | solution.py:13
  266.6 5.8 %copy-start = (bf16[2048,2048]{1,0:T(8,128)(2,1)S(1)}, bf16[2048,2048]{1,0:T(8,128)(2,1)}, u32[]{:S(2)}) copy-start(bf16[2048,2048]{1,0:T(8,128)(2,1)} %get-tuple-element.502) | copy-start | bytes 25165828 | tf_op jit(solution)/shard_map/while/body/eval_jaxpr/cond
  275.0 9.1 %collective-permute-start.1 = (bf16[32,2048]{1,0:T(8,128)(2,1)S(1)}, bf16[32,2048]{1,0:T(8,128)(2,1)S(1)}, u32[]{:S(2)}, u32[]{:S(2)}) collective-permute-start(bf16[32,2048]{1,0:T(8,128)(2,1)S(1)} %get-tuple-element.701), channel_id=1, source_target_pairs={{4,0},{8,4},{12,8},{16,12},{20,16},{24,20},{28,24},{5,1},{9,5},{13... | collective-permute-start | bytes 393224 | tf_op jit(solution)/shard_map/while/body/eval_jaxpr/ppermute | solution.py:13
  284.1 5.8 %copy-start = (bf16[2048,2048]{1,0:T(8,128)(2,1)S(1)}, bf16[2048,2048]{1,0:T(8,128)(2,1)}, u32[]{:S(2)}) copy-start(bf16[2048,2048]{1,0:T(8,128)(2,1)} %get-tuple-element.502) | copy-start | bytes 25165828 | tf_op jit(solution)/shard_map/while/body/eval_jaxpr/cond
  292.5 8.5 %collective-permute-start.1 = (bf16[32,2048]{1,0:T(8,128)(2,1)S(1)}, bf16[32,2048]{1,0:T(8,128)(2,1)S(1)}, u32[]{:S(2)}, u32[]{:S(2)}) collective-permute-start(bf16[32,2048]{1,0:T(8,128)(2,1)S(1)} %get-tuple-element.701), channel_id=1, source_target_pairs={{4,0},{8,4},{12,8},{16,12},{20,16},{24,20},{28,24},{5,1},{9,5},{13... | collective-permute-start | bytes 393224 | tf_op jit(solution)/shard_map/while/body/eval_jaxpr/ppermute | solution.py:13
  300.9 5.8 %copy-start = (bf16[2048,2048]{1,0:T(8,128)(2,1)S(1)}, bf16[2048,2048]{1,0:T(8,128)(2,1)}, u32[]{:S(2)}) copy-start(bf16[2048,2048]{1,0:T(8,128)(2,1)} %get-tuple-element.502) | copy-start | bytes 25165828 | tf_op jit(solution)/shard_map/while/body/eval_jaxpr/cond
  309.3 7.5 %collective-permute-start.1 = (bf16[32,2048]{1,0:T(8,128)(2,1)S(1)}, bf16[32,2048]{1,0:T(8,128)(2,1)S(1)}, u32[]{:S(2)}, u32[]{:S(2)}) collective-permute-start(bf16[32,2048]{1,0:T(8,128)(2,1)S(1)} %get-tuple-element.701), channel_id=1, source_target_pairs={{4,0},{8,4},{12,8},{16,12},{20,16},{24,20},{28,24},{5,1},{9,5},{13... | collective-permute-start | bytes 393224 | tf_op jit(solution)/shard_map/while/body/eval_jaxpr/ppermute | solution.py:13
  316.8 5.8 %copy-start = (bf16[2048,2048]{1,0:T(8,128)(2,1)S(1)}, bf16[2048,2048]{1,0:T(8,128)(2,1)}, u32[]{:S(2)}) copy-start(bf16[2048,2048]{1,0:T(8,128)(2,1)} %get-tuple-element.502) | copy-start | bytes 25165828 | tf_op jit(solution)/shard_map/while/body/eval_jaxpr/cond
  325.1 6.9 %collective-permute-start.1 = (bf16[32,2048]{1,0:T(8,128)(2,1)S(1)}, bf16[32,2048]{1,0:T(8,128)(2,1)S(1)}, u32[]{:S(2)}, u32[]{:S(2)}) collective-permute-start(bf16[32,2048]{1,0:T(8,128)(2,1)S(1)} %get-tuple-element.701), channel_id=1, source_target_pairs={{4,0},{8,4},{12,8},{16,12},{20,16},{24,20},{28,24},{5,1},{9,5},{13... | collective-permute-start | bytes 393224 | tf_op jit(solution)/shard_map/while/body/eval_jaxpr/ppermute | solution.py:13
  332.0 5.6 %copy-start.4 = (bf16[4,32,2048]{2,1,0:T(8,128)(2,1)}, bf16[4,32,2048]{2,1,0:T(8,128)(2,1)S(1)}, u32[]{:S(2)}) copy-start(bf16[4,32,2048]{2,1,0:T(8,128)(2,1)S(1)} %get-tuple-element.527) | copy-start | bytes 1572868
  (5 other events, 12.5 us)
Sparse Core Ops, SparseCore 0:
  9.5 31.9 all-gather.4
  43.1 58.2 all-gather.6
  184.7 35.6 reduce-scatter.6
  337.8 68.5 reduce-scatter.4
where the time goes:
time: 423 us; the launch traced here: 422 us
  waiting for transfers between devices  295 us (70%)
  matrix products  63.1 us (15%)
  starting transfers between devices  28.5 us (7%)
  local copies, waits for them, and re-layouts  17.2 us (4%)
  between operations  13.8 us (3%)
  other arithmetic  4.26 us (1%)
    ppermute x22, waiting for transfers between devices, shifted(): return lax.ppermute(block, axis, route)  195 us
    reduce_scatter x1, waiting for transfers between devices, t5_weight_total(): lax.psum_scatter((lax.dot_general(input_flat, local_flat, (((0,), (0,)),...  65.3 us
    dot_general x8, matrix products, layer_back(): preact = jnp.dot(saved_input, weight, preferred_element_type=jnp.float32)  34.3 us
    all_gather x1, waiting for transfers between devices, shards(): lax.all_gather(vit_weight[0], 'dp', axis=0, tiled=True)  32.8 us
    ppermute x22, starting transfers between devices, shifted(): return lax.ppermute(block, axis, route)  28.4 us
    dot_general x8, matrix products, layer_back(): lax.dot_general(local_grad, weight, (((1,), (1,)), ((), ())), preferred_e...  21.1 us
    unnamed x10, local copies, waits for them, and re-layouts  12.9 us
  transfers between devices with their start and end apart: 26, of which 24 were waited for; matrix products, arithmetic and copies ran while one was open for 17% of the time, Pallas kernels for 0%

commit v1 on v0

v1 whole, which is shorter than its diff:
```python
import jax
import jax.numpy as jnp
from jax import lax
from jax.sharding import PartitionSpec as P

root_half = 0.7071067811865476
inv_root_tau = 0.3989422804014327


def shifted(block, axis, distance):
    devices = range(lax.axis_size(axis))
    route = [(i - distance, i) for i in devices if i - distance in devices]
    return lax.ppermute(block, axis, route)


def gelu_slope(preact):
    cumulative = 0.5 * (1.0 + lax.erf(preact * root_half))
    density = jnp.exp(-0.5 * preact * preact) * inv_root_tau
    return cumulative + preact * density


def slopes(saved, weight):
    flat = saved.reshape(-1, saved.shape[-1])
    return gelu_slope(jnp.dot(flat, weight, preferred_element_type=jnp.float32)).reshape(saved.shape)


def token_columns(saved):
    flat = saved.reshape(-1, saved.shape[-1])
    parts = lax.axis_size("dp")
    split = flat.reshape(flat.shape[0], parts, -1).transpose(1, 0, 2)
    return lax.all_to_all(split, "dp", 0, 0, tiled=True)


def weight_rows(columns, locals_all, scale):
    total = jnp.zeros((columns.shape[2], locals_all.shape[2]), jnp.float32)
    for group in range(columns.shape[0]):
        term = lax.dot_general(
            columns[group], locals_all[group], (((0,), (0,)), ((), ())),
            preferred_element_type=jnp.float32,
        )
        total = total + (term * scale).astype(jnp.bfloat16).astype(jnp.float32)
    return total


def shards(vit_weight, t5_weight, vit_saved, t5_saved, vit_top_grad, t5_top_grad):
    section_count = lax.axis_size("section")
    section_index = lax.axis_index("section")
    is_last = section_index == section_count - 1
    depth = section_count - 1 - section_index
    weights = [lax.all_gather(w[0], "dp", axis=0, tiled=True) for w in (t5_weight, vit_weight)]
    saved = [t5_saved[0], vit_saved[0]]
    tops = [t5_top_grad, vit_top_grad]
    columns = [token_columns(s) for s in saved]
    slope = [slopes(s, w) for s, w in zip(saved, weights)]
    micro_count, token_count = saved[0].shape[:2]
    scale = 1.0 / (micro_count * token_count)

    def tick(index, state):
        micro = index - depth
        active = jnp.logical_and(micro >= 0, micro < micro_count)
        slot = jnp.clip(micro, 0, micro_count - 1)

        def advance(operands):
            result = []
            for (received, grads, locals_now), w, top, sl in zip(operands, weights, tops, slope):
                above = jnp.where(is_last, top[slot], received)
                upper = above.astype(jnp.float32)
                local = (upper * sl[slot]).astype(jnp.bfloat16)
                through = lax.dot_general(
                    local, w, (((1,), (1,)), ((), ())), preferred_element_type=jnp.float32
                )
                below = (upper + through).astype(jnp.bfloat16)
                result.append((
                    below,
                    lax.dynamic_update_index_in_dim(grads, below, slot, 0),
                    lax.dynamic_update_index_in_dim(locals_now, local, slot, 0),
                ))
            return tuple(result)

        state = lax.cond(active, advance, lambda operands: operands, state)
        return tuple((shifted(a, "section", -1), b, c) for a, b, c in state)

    start = tuple(
        (jnp.zeros_like(top[0]), jnp.zeros_like(s), jnp.zeros_like(s)) for top, s in zip(tops, saved)
    )
    state = lax.fori_loop(0, section_count + micro_count - 1, tick, start)
    sums = []
    for (_, _, locals_now), cols in zip(state, columns):
        flat = locals_now.reshape(-1, locals_now.shape[-1])
        everyone = lax.all_gather(flat, "dp", axis=0, tiled=False)
        sums.append(weight_rows(cols, everyone, scale))
    return (state[1][1][None], state[0][1][None], sums[1][None], sums[0][None])


def solution(mesh):
    placed = (
        P("section", "dp", None),
        P("section", "dp", None),
        P("section", None, "dp", None),
        P("section", None, "dp", None),
        P(None, "dp", None),
        P(None, "dp", None),
    )
    return jax.shard_map(
        shards,
        mesh=mesh,
        in_specs=placed,
        out_specs=(
            P("section", None, "dp", None),
            P("section", None, "dp", None),
            P("section", "dp", None),
            P("section", "dp", None),
        ),
        check_vma=False,
    )
```

time: 423 us -> 395 us (0.934)
  waiting for transfers between devices: 295 us -> 255 us
  starting transfers between devices: 28.5 us -> 36.1 us
  other arithmetic: 4.26 us -> 9.35 us
  matrix products: 63.1 us -> 58.6 us
    all_gather x2 -> x4, waiting for transfers between devices: 32.9 us -> 104 us  [the longest x2 89.2 us: shards(): lax.all_gather(w[0], 'dp', axis=0, tiled=True)]
    reduce_scatter x1 -> x0, waiting for transfers between devices: 65.3 us -> none  [t5_weight_total(): lax.psum_scatter((lax.dot_general(input_flat, local_flat, (((0,), (0,)),...]
    ppermute x22, waiting for transfers between devices: 195 us -> 135 us  [shifted(): return lax.ppermute(block, axis, route)]
    all_to_all x0 -> x2, waiting for transfers between devices: none -> 13.3 us  [token_columns(): return lax.all_to_all(split, 'dp', 0, 0, tiled=True)]
    dynamic_update_slice x0 -> x8, other arithmetic: none -> 9.35 us  [advance(): lax.dynamic_update_index_in_dim(locals_now, local, slot, 0)]
    all_to_all x0 -> x2, starting transfers between devices: none -> 7.63 us  [token_columns(): return lax.all_to_all(split, 'dp', 0, 0, tiled=True)]
    unnamed x10 -> x15, local copies, waits for them, and re-layouts: 12.9 us -> 5.37 us
    cond x16 -> x30, local copies, waits for them, and re-layouts: 2.51 us -> 8.99 us
  transfers between devices with their start and end apart: 26 -> 28, of which waited for: 24 -> 16; matrix products, arithmetic and copies ran while one was open for 17% -> 3% of each run, Pallas kernels for 0% -> 0%
where the time goes in v1:
time: 395 us; the launch traced here: 394 us
  waiting for transfers between devices  255 us (65%)
  matrix products  58.6 us (15%)
  starting transfers between devices  36.1 us (9%)
  local copies, waits for them, and re-layouts  21.2 us (5%)
  between operations  13.9 us (4%)
  other arithmetic  9.35 us (2%)
    ppermute x22, waiting for transfers between devices, shifted(): return lax.ppermute(block, axis, route)  135 us
    all_gather x2, waiting for transfers between devices, shards(): lax.all_gather(w[0], 'dp', axis=0, tiled=True)  89.2 us
    dot_general x8, matrix products, advance(): lax.dot_general(local, w, (((1,), (1,)), ((), ())), preferred_element_typ...  34.7 us
    ppermute x22, starting transfers between devices, shifted(): return lax.ppermute(block, axis, route)  28.3 us
    all_gather x2, waiting for transfers between devices, shards(): everyone = lax.all_gather(flat, 'dp', axis=0, tiled=False)  15.2 us
    dot_general x8, matrix products, weight_rows(): lax.dot_general(columns[group], locals_all[group], (((0,), (0,)), ((), ()...  14.1 us
    all_to_all x2, waiting for transfers between devices, token_columns(): return lax.all_to_all(split, 'dp', 0, 0, tiled=True)  13.3 us
    dot_general x2, matrix products, slopes(): jnp.dot(flat, weight, preferred_element_type=jnp.float32)  9.78 us
  transfers between devices with their start and end apart: 28, of which 16 were waited for; matrix products, arithmetic and copies ran while one was open for 3% of the time, Pallas kernels for 0%

profile of v1, /device:TPU:0, one launch (start us, length us, event | category | flops | bytes accessed | tf_op | source)
XLA Modules:
  0.0 394.1 jit_solution(15382990463806078175)
XLA Ops:
  8.7 32.8 %all-gather.13.cloned.1.call-done = bf16[1,1280,1280]{2,1,0:T(8,128)(2,1)} async-done(((bf16[1,320,1280]{2,1,0:T(8,128)(2,1)}), bf16[1,1280,1280]{2,1,0:T(8,128)(2,1)}) %all-gather.13.cloned.1.call-update) | async-done | bytes 3276816 | tf_op jit(solution)/shard_map/all_gather | solution.py:50
  41.6 3.5 fusion.25
  45.1 56.3 %all-gather.11.cloned.1.call-done = bf16[1,2048,2048]{2,1,0:T(8,128)(2,1)} async-done(((bf16[1,512,2048]{2,1,0:T(8,128)(2,1)}), bf16[1,2048,2048]{2,1,0:T(8,128)(2,1)}) %all-gather.11.cloned.1.call-update) | async-done | bytes 8388624 | tf_op jit(solution)/shard_map/all_gather | solution.py:50
  101.4 6.3 %fusion.21 = f32[128,2048]{1,0:T(8,128)} fusion(bf16[128,2048]{1,0:T(8,128)(2,1)} %bitcast.137, bf16[1,2048,2048]{2,1,0:T(8,128)(2,1)} %all-gather.11.cloned.1.call-done), kind=kOutput, calls=%fused_computation.39 | convolution fusion | flops 1075838976 | bytes 9961472 | tf_op jit(solution)/shard_map/dot_general | solution.py:24
  110.9 216.5 %while.23 = (s32[]{:T(128)}, bf16[32,2048]{1,0:T(8,128)(2,1)S(1)}, bf16[4,32,2048]{2,1,0:T(8,128)(2,1)}, bf16[4,32,2048]{2,1,0:T(8,128)(2,1)}, bf16[32,1280]{1,0...) while((s32[]{:T(128)}, bf16[32,2048]{1,0:T(8,128)(2,1)S(1)}, ...), condition=%wide.region_3.4_spmd, body=%wide.region_0.3_spmd.sunk | while | flops 374571008 | bytes 19224132 | solution.py:86
  114.8 6.9 %collective-permute-done.1 = bf16[32,1280]{1,0:T(8,128)(2,1)S(1)} collective-permute-done((bf16[32,1280]{1,0:T(8,128)(2,1)}, bf16[32,1280]{1,0:T(8,128)(2,1)S(1)}, u32[]{:S(2)}, u32[]{:S(2)}) %collective-permute-start.1) | collective-permute-done | bytes 81952 | tf_op jit(solution)/shard_map/while/body/eval_jaxpr/ppermute | solution.py:13
  125.6 6.8 %collective-permute-done.1 = bf16[32,1280]{1,0:T(8,128)(2,1)S(1)} collective-permute-done((bf16[32,1280]{1,0:T(8,128)(2,1)}, bf16[32,1280]{1,0:T(8,128)(2,1)S(1)}, u32[]{:S(2)}, u32[]{:S(2)}) %collective-permute-start.1) | collective-permute-done | bytes 81952 | tf_op jit(solution)/shard_map/while/body/eval_jaxpr/ppermute | solution.py:13
  136.3 6.9 %collective-permute-done.1 = bf16[32,1280]{1,0:T(8,128)(2,1)S(1)} collective-permute-done((bf16[32,1280]{1,0:T(8,128)(2,1)}, bf16[32,1280]{1,0:T(8,128)(2,1)S(1)}, u32[]{:S(2)}, u32[]{:S(2)}) %collective-permute-start.1) | collective-permute-done | bytes 81952 | tf_op jit(solution)/shard_map/while/body/eval_jaxpr/ppermute | solution.py:13
  147.1 7.1 %collective-permute-done.1 = bf16[32,1280]{1,0:T(8,128)(2,1)S(1)} collective-permute-done((bf16[32,1280]{1,0:T(8,128)(2,1)}, bf16[32,1280]{1,0:T(8,128)(2,1)S(1)}, u32[]{:S(2)}, u32[]{:S(2)}) %collective-permute-start.1) | collective-permute-done | bytes 81952 | tf_op jit(solution)/shard_map/while/body/eval_jaxpr/ppermute | solution.py:13
  158.1 6.6 %collective-permute-done.1 = bf16[32,1280]{1,0:T(8,128)(2,1)S(1)} collective-permute-done((bf16[32,1280]{1,0:T(8,128)(2,1)}, bf16[32,1280]{1,0:T(8,128)(2,1)S(1)}, u32[]{:S(2)}, u32[]{:S(2)}) %collective-permute-start.1) | collective-permute-done | bytes 81952 | tf_op jit(solution)/shard_map/while/body/eval_jaxpr/ppermute | solution.py:13
  168.6 6.7 %collective-permute-done.1 = bf16[32,1280]{1,0:T(8,128)(2,1)S(1)} collective-permute-done((bf16[32,1280]{1,0:T(8,128)(2,1)}, bf16[32,1280]{1,0:T(8,128)(2,1)S(1)}, u32[]{:S(2)}, u32[]{:S(2)}) %collective-permute-start.1) | collective-permute-done | bytes 81952 | tf_op jit(solution)/shard_map/while/body/eval_jaxpr/ppermute | solution.py:13
  179.1 67.6 %collective-permute-done.1 = bf16[32,1280]{1,0:T(8,128)(2,1)S(1)} collective-permute-done((bf16[32,1280]{1,0:T(8,128)(2,1)}, bf16[32,1280]{1,0:T(8,128)(2,1)S(1)}, u32[]{:S(2)}, u32[]{:S(2)}) %collective-permute-start.1) | collective-permute-done | bytes 81952 | tf_op jit(solution)/shard_map/while/body/eval_jaxpr/ppermute | solution.py:13
  246.8 11.0 %conditional.2 = (bf16[32,2048]{1,0:T(8,128)(2,1)}, bf16[4,32,2048]{2,1,0:T(8,128)(2,1)}, bf16[4,32,2048]{2,1,0:T(8,128)(2,1)}, bf16[32,1280]{1,0:T(8,128)(2,1)}...) conditional(s32[]{:T(128)} %convert_element_type.202, (bf16[32,2048]{1,0:T(8,128)(2,1)S(1)}, ...), branch_computations={%region_1.1_spmd, %region_2.2_spmd} | conditional | flops 374571008 | bytes 18371720 | solution.py:80
  246.8 6.9 %bitcast_dynamic-update-slice_fusion.1 = (bf16[4,32,2048]{2,1,0:T(8,128)(2,1)}, bf16[32,2048]{1,0:T(8,128)(2,1)}) fusion(bf16[4,32,2048]{2,1,0:T(8,128)(2,1)} %get-tuple-element.315, s32[]{:T(128)S(6)} %min.9, bf16[2048,2048]{1,0:T(8,128)(2,1)} %get-tuple-element.314, f32[4,32,2048]{2,1,0:T(8,128)} %get-tuple-element.313, ...), kind=kOutput, calls=%fused_computation.9 | convolution fusion | flops 268959744 | bytes 9439232 | tf_op jit(solution)/shard_map/while/body/eval_jaxpr/cond/branch_1_fun/dot_general | solution.py:69
  260.4 7.1 %collective-permute-done.1 = bf16[32,1280]{1,0:T(8,128)(2,1)S(1)} collective-permute-done((bf16[32,1280]{1,0:T(8,128)(2,1)}, bf16[32,1280]{1,0:T(8,128)(2,1)S(1)}, u32[]{:S(2)}, u32[]{:S(2)}) %collective-permute-start.1) | collective-permute-done | bytes 81952 | tf_op jit(solution)/shard_map/while/body/eval_jaxpr/ppermute | solution.py:13
  267.4 11.0 %conditional.2 = (bf16[32,2048]{1,0:T(8,128)(2,1)}, bf16[4,32,2048]{2,1,0:T(8,128)(2,1)}, bf16[4,32,2048]{2,1,0:T(8,128)(2,1)}, bf16[32,1280]{1,0:T(8,128)(2,1)}...) conditional(s32[]{:T(128)} %convert_element_type.202, (bf16[32,2048]{1,0:T(8,128)(2,1)S(1)}, ...), branch_computations={%region_1.1_spmd, %region_2.2_spmd} | conditional | flops 374571008 | bytes 18371720 | solution.py:80
  267.4 6.9 %bitcast_dynamic-update-slice_fusion.1 = (bf16[4,32,2048]{2,1,0:T(8,128)(2,1)}, bf16[32,2048]{1,0:T(8,128)(2,1)}) fusion(bf16[4,32,2048]{2,1,0:T(8,128)(2,1)} %get-tuple-element.315, s32[]{:T(128)S(6)} %min.9, bf16[2048,2048]{1,0:T(8,128)(2,1)} %get-tuple-element.314, f32[4,32,2048]{2,1,0:T(8,128)} %get-tuple-element.313, ...), kind=kOutput, calls=%fused_computation.9 | convolution fusion | flops 268959744 | bytes 9439232 | tf_op jit(solution)/shard_map/while/body/eval_jaxpr/cond/branch_1_fun/dot_general | solution.py:69
  281.0 6.5 %collective-permute-done.1 = bf16[32,1280]{1,0:T(8,128)(2,1)S(1)} collective-permute-done((bf16[32,1280]{1,0:T(8,128)(2,1)}, bf16[32,1280]{1,0:T(8,128)(2,1)S(1)}, u32[]{:S(2)}, u32[]{:S(2)}) %collective-permute-start.1) | collective-permute-done | bytes 81952 | tf_op jit(solution)/shard_map/while/body/eval_jaxpr/ppermute | solution.py:13
  287.5 11.0 %conditional.2 = (bf16[32,2048]{1,0:T(8,128)(2,1)}, bf16[4,32,2048]{2,1,0:T(8,128)(2,1)}, bf16[4,32,2048]{2,1,0:T(8,128)(2,1)}, bf16[32,1280]{1,0:T(8,128)(2,1)}...) conditional(s32[]{:T(128)} %convert_element_type.202, (bf16[32,2048]{1,0:T(8,128)(2,1)S(1)}, ...), branch_computations={%region_1.1_spmd, %region_2.2_spmd} | conditional | flops 374571008 | bytes 18371720 | solution.py:80
  287.6 6.9 %bitcast_dynamic-update-slice_fusion.1 = (bf16[4,32,2048]{2,1,0:T(8,128)(2,1)}, bf16[32,2048]{1,0:T(8,128)(2,1)}) fusion(bf16[4,32,2048]{2,1,0:T(8,128)(2,1)} %get-tuple-element.315, s32[]{:T(128)S(6)} %min.9, bf16[2048,2048]{1,0:T(8,128)(2,1)} %get-tuple-element.314, f32[4,32,2048]{2,1,0:T(8,128)} %get-tuple-element.313, ...), kind=kOutput, calls=%fused_computation.9 | convolution fusion | flops 268959744 | bytes 9439232 | tf_op jit(solution)/shard_map/while/body/eval_jaxpr/cond/branch_1_fun/dot_general | solution.py:69
  301.2 6.8 %collective-permute-done.1 = bf16[32,1280]{1,0:T(8,128)(2,1)S(1)} collective-permute-done((bf16[32,1280]{1,0:T(8,128)(2,1)}, bf16[32,1280]{1,0:T(8,128)(2,1)S(1)}, u32[]{:S(2)}, u32[]{:S(2)}) %collective-permute-start.1) | collective-permute-done | bytes 81952 | tf_op jit(solution)/shard_map/while/body/eval_jaxpr/ppermute | solution.py:13
  307.9 11.0 %conditional.2 = (bf16[32,2048]{1,0:T(8,128)(2,1)}, bf16[4,32,2048]{2,1,0:T(8,128)(2,1)}, bf16[4,32,2048]{2,1,0:T(8,128)(2,1)}, bf16[32,1280]{1,0:T(8,128)(2,1)}...) conditional(s32[]{:T(128)} %convert_element_type.202, (bf16[32,2048]{1,0:T(8,128)(2,1)S(1)}, ...), branch_computations={%region_1.1_spmd, %region_2.2_spmd} | conditional | flops 374571008 | bytes 18371720 | solution.py:80
  308.0 6.9 %bitcast_dynamic-update-slice_fusion.1 = (bf16[4,32,2048]{2,1,0:T(8,128)(2,1)}, bf16[32,2048]{1,0:T(8,128)(2,1)}) fusion(bf16[4,32,2048]{2,1,0:T(8,128)(2,1)} %get-tuple-element.315, s32[]{:T(128)S(6)} %min.9, bf16[2048,2048]{1,0:T(8,128)(2,1)} %get-tuple-element.314, f32[4,32,2048]{2,1,0:T(8,128)} %get-tuple-element.313, ...), kind=kOutput, calls=%fused_computation.9 | convolution fusion | flops 268959744 | bytes 9439232 | tf_op jit(solution)/shard_map/while/body/eval_jaxpr/cond/branch_1_fun/dot_general | solution.py:69
  321.6 5.9 %collective-permute-done.1 = bf16[32,1280]{1,0:T(8,128)(2,1)S(1)} collective-permute-done((bf16[32,1280]{1,0:T(8,128)(2,1)}, bf16[32,1280]{1,0:T(8,128)(2,1)S(1)}, u32[]{:S(2)}, u32[]{:S(2)}) %collective-permute-start.1) | collective-permute-done | bytes 81952 | tf_op jit(solution)/shard_map/while/body/eval_jaxpr/ppermute | solution.py:13
  330.5 3.5 all-to-all-start
  335.2 9.3 %all-to-all-done = bf16[4,128,320]{1,2,0:T(8,128)(2,1)S(1)} async-done(((bf16[4,128,320]{1,2,0:T(8,128)(2,1)}), bf16[4,128,320]{1,2,0:T(8,128)(2,1)S(1)}, u32[]{:S(2)}, u32[]{:S(2)}) %all-to-all-start) | async-done | bytes 327712 | tf_op jit(solution)/shard_map/all_to_all | solution.py:31
  344.5 4.2 %all-to-all-start.1 = ((bf16[4,128,512]{2,1,0:T(8,128)(2,1)}), bf16[4,128,512]{2,1,0:T(8,128)(2,1)}, u32[]{:S(2)}, u32[]{:S(2)}) async-start(bf16[4,128,512]{2,1,0:T(8,128)(2,1)} %copy.22), calls=%async_computation.1 | async-start | bytes 1048576 | tf_op jit(solution)/shard_map/all_to_all | solution.py:31
  353.4 4.1 %all-to-all-done.1 = bf16[4,128,512]{2,1,0:T(8,128)(2,1)} async-done(((bf16[4,128,512]{2,1,0:T(8,128)(2,1)}), bf16[4,128,512]{2,1,0:T(8,128)(2,1)}, u32[]{:S(2)}, u32[]{:S(2)}) %all-to-all-start.1) | async-done | bytes 524320 | tf_op jit(solution)/shard_map/all_to_all | solution.py:31
  357.5 15.2 %all-gather.9.cloned.1.call-done = bf16[4,128,2048]{2,1,0:T(8,128)(2,1)} async-done(((bf16[1,128,2048]{2,1,0:T(8,128)(2,1)}), bf16[4,128,2048]{2,1,0:T(8,128)(2,1)}) %all-gather.9.cloned.1.call-update) | async-done | bytes 2097168 | tf_op jit(solution)/shard_map/all_gather | solution.py:90
  372.7 1.9 multiply_convert_fusion
  378.0 4.2 %add_bitcast_fusion = f32[1,512,2048]{1,2,0:T(8,128)} fusion(bf16[2048,512]{1,0:T(8,128)(2,1)S(1)} %multiply_convert_fusion, bf16[2048,512]{1,0:T(8,128)(2,1)S(1)} %multiply_convert_fusion.1, bf16[2048,512]{1,0:T(8,128)(2,1)S(1)} %multiply_convert_fusion.2, bf16[4,128,2048]{2,1,0:T(8,128)(2,1)S(1)} %copy-done.3, bf16[4,128,512]{2,1,0:T(8,128)(2,1)} %all-to-all-done.1), kind=kOutput, calls=%fused_computation.14 | convolution fusion | flops 277872640 | bytes 11141120 | tf_op jit(solution)/shard_map/dot_general | solution.py:37
  382.2 5.3 %copy.23 = f32[1,512,2048]{2,1,0:T(8,128)} copy(f32[1,512,2048]{1,2,0:T(8,128)} %add_bitcast_fusion) | data formatting | bytes 8388608
  (121 shorter events, 79.7 us)
Async XLA Ops:
  7.2 34.4 %copy-start.8 = (bf16[1,4,32,1280]{3,2,1,0:T(8,128)(2,1)S(1)}, bf16[1,4,32,1280]{3,2,1,0:T(8,128)(2,1)}, u32[]{:S(2)}) copy-start(bf16[1,4,32,1280]{3,2,1,0:T(8,128)(2,1)} %param.12) | copy-start | bytes 983044
  7.2 34.4 %all-gather.13.cloned.1.call-start = ((), (), s32[]{:S(2)}) async-start(), calls=%async_computation.5 | async-start | bytes 4096000 | tf_op jit(solution)/shard_map/all_gather | solution.py:50
  7.9 93.5 %all-gather.11.cloned.1.call-start = ((), (), s32[]{:S(2)}) async-start(), calls=%async_computation.4 | async-start | bytes 10485760 | tf_op jit(solution)/shard_map/all_gather | solution.py:50
  8.7 340.0 %all-gather.7.cloned.1.call-start = ((), (), s32[]{:S(2)}) async-start(), calls=%async_computation.2 | async-start | bytes 1638400 | tf_op jit(solution)/shard_map/all_gather | solution.py:90
  101.4 9.5 %copy-start = (bf16[1,1280,1280]{2,1,0:T(8,128)(2,1)S(1)}, bf16[1,1280,1280]{2,1,0:T(8,128)(2,1)}, u32[]{:S(2)}) copy-start(bf16[1,1280,1280]{2,1,0:T(8,128)(2,1)} %all-gather.13.cloned.1.call-done) | copy-start | bytes 9830404
  112.2 9.5 %collective-permute-start = (bf16[32,2048]{1,0:T(8,128)(2,1)}, bf16[32,2048]{1,0:T(8,128)(2,1)S(1)}, u32[]{:S(2)}, u32[]{:S(2)}) collective-permute-start(bf16[32,2048]{1,0:T(8,128)(2,1)} %get-tuple-element.504), channel_id=1, source_target_pairs={{4,0},{8,4},{12,8},{16,12},{20,16},{24,20},{28,24},{5,1},{9,5},{13... | collective-permute-start | bytes 393224 | tf_op jit(solution)/shard_map/while/body/eval_jaxpr/ppermute | solution.py:13
  113.5 8.2 %collective-permute-start.1 = (bf16[32,1280]{1,0:T(8,128)(2,1)}, bf16[32,1280]{1,0:T(8,128)(2,1)S(1)}, u32[]{:S(2)}, u32[]{:S(2)}) collective-permute-start(bf16[32,1280]{1,0:T(8,128)(2,1)} %get-tuple-element.507), channel_id=1, source_target_pairs={{4,0},{8,4},{12,8},{16,12},{20,16},{24,20},{28,24},{5,1},{9,5},{13... | collective-permute-start | bytes 245768 | tf_op jit(solution)/shard_map/while/body/eval_jaxpr/ppermute | solution.py:13
  123.0 9.4 %collective-permute-start = (bf16[32,2048]{1,0:T(8,128)(2,1)}, bf16[32,2048]{1,0:T(8,128)(2,1)S(1)}, u32[]{:S(2)}, u32[]{:S(2)}) collective-permute-start(bf16[32,2048]{1,0:T(8,128)(2,1)} %get-tuple-element.504), channel_id=1, source_target_pairs={{4,0},{8,4},{12,8},{16,12},{20,16},{24,20},{28,24},{5,1},{9,5},{13... | collective-permute-start | bytes 393224 | tf_op jit(solution)/shard_map/while/body/eval_jaxpr/ppermute | solution.py:13
  124.3 8.1 %collective-permute-start.1 = (bf16[32,1280]{1,0:T(8,128)(2,1)}, bf16[32,1280]{1,0:T(8,128)(2,1)S(1)}, u32[]{:S(2)}, u32[]{:S(2)}) collective-permute-start(bf16[32,1280]{1,0:T(8,128)(2,1)} %get-tuple-element.507), channel_id=1, source_target_pairs={{4,0},{8,4},{12,8},{16,12},{20,16},{24,20},{28,24},{5,1},{9,5},{13... | collective-permute-start | bytes 245768 | tf_op jit(solution)/shard_map/while/body/eval_jaxpr/ppermute | solution.py:13
  133.7 9.5 %collective-permute-start = (bf16[32,2048]{1,0:T(8,128)(2,1)}, bf16[32,2048]{1,0:T(8,128)(2,1)S(1)}, u32[]{:S(2)}, u32[]{:S(2)}) collective-permute-start(bf16[32,2048]{1,0:T(8,128)(2,1)} %get-tuple-element.504), channel_id=1, source_target_pairs={{4,0},{8,4},{12,8},{16,12},{20,16},{24,20},{28,24},{5,1},{9,5},{13... | collective-permute-start | bytes 393224 | tf_op jit(solution)/shard_map/while/body/eval_jaxpr/ppermute | solution.py:13
  135.0 8.2 %collective-permute-start.1 = (bf16[32,1280]{1,0:T(8,128)(2,1)}, bf16[32,1280]{1,0:T(8,128)(2,1)S(1)}, u32[]{:S(2)}, u32[]{:S(2)}) collective-permute-start(bf16[32,1280]{1,0:T(8,128)(2,1)} %get-tuple-element.507), channel_id=1, source_target_pairs={{4,0},{8,4},{12,8},{16,12},{20,16},{24,20},{28,24},{5,1},{9,5},{13... | collective-permute-start | bytes 245768 | tf_op jit(solution)/shard_map/while/body/eval_jaxpr/ppermute | solution.py:13
  144.5 9.7 %collective-permute-start = (bf16[32,2048]{1,0:T(8,128)(2,1)}, bf16[32,2048]{1,0:T(8,128)(2,1)S(1)}, u32[]{:S(2)}, u32[]{:S(2)}) collective-permute-start(bf16[32,2048]{1,0:T(8,128)(2,1)} %get-tuple-element.504), channel_id=1, source_target_pairs={{4,0},{8,4},{12,8},{16,12},{20,16},{24,20},{28,24},{5,1},{9,5},{13... | collective-permute-start | bytes 393224 | tf_op jit(solution)/shard_map/while/body/eval_jaxpr/ppermute | solution.py:13
  145.8 8.4 %collective-permute-start.1 = (bf16[32,1280]{1,0:T(8,128)(2,1)}, bf16[32,1280]{1,0:T(8,128)(2,1)S(1)}, u32[]{:S(2)}, u32[]{:S(2)}) collective-permute-start(bf16[32,1280]{1,0:T(8,128)(2,1)} %get-tuple-element.507), channel_id=1, source_target_pairs={{4,0},{8,4},{12,8},{16,12},{20,16},{24,20},{28,24},{5,1},{9,5},{13... | collective-permute-start | bytes 245768 | tf_op jit(solution)/shard_map/while/body/eval_jaxpr/ppermute | solution.py:13
  155.5 9.2 %collective-permute-start = (bf16[32,2048]{1,0:T(8,128)(2,1)}, bf16[32,2048]{1,0:T(8,128)(2,1)S(1)}, u32[]{:S(2)}, u32[]{:S(2)}) collective-permute-start(bf16[32,2048]{1,0:T(8,128)(2,1)} %get-tuple-element.504), channel_id=1, source_target_pairs={{4,0},{8,4},{12,8},{16,12},{20,16},{24,20},{28,24},{5,1},{9,5},{13... | collective-permute-start | bytes 393224 | tf_op jit(solution)/shard_map/while/body/eval_jaxpr/ppermute | solution.py:13
  156.8 7.9 %collective-permute-start.1 = (bf16[32,1280]{1,0:T(8,128)(2,1)}, bf16[32,1280]{1,0:T(8,128)(2,1)S(1)}, u32[]{:S(2)}, u32[]{:S(2)}) collective-permute-start(bf16[32,1280]{1,0:T(8,128)(2,1)} %get-tuple-element.507), channel_id=1, source_target_pairs={{4,0},{8,4},{12,8},{16,12},{20,16},{24,20},{28,24},{5,1},{9,5},{13... | collective-permute-start | bytes 245768 | tf_op jit(solution)/shard_map/while/body/eval_jaxpr/ppermute | solution.py:13
  166.0 9.3 %collective-permute-start = (bf16[32,2048]{1,0:T(8,128)(2,1)}, bf16[32,2048]{1,0:T(8,128)(2,1)S(1)}, u32[]{:S(2)}, u32[]{:S(2)}) collective-permute-start(bf16[32,2048]{1,0:T(8,128)(2,1)} %get-tuple-element.504), channel_id=1, source_target_pairs={{4,0},{8,4},{12,8},{16,12},{20,16},{24,20},{28,24},{5,1},{9,5},{13... | collective-permute-start | bytes 393224 | tf_op jit(solution)/shard_map/while/body/eval_jaxpr/ppermute | solution.py:13
  167.3 8.0 %collective-permute-start.1 = (bf16[32,1280]{1,0:T(8,128)(2,1)}, bf16[32,1280]{1,0:T(8,128)(2,1)S(1)}, u32[]{:S(2)}, u32[]{:S(2)}) collective-permute-start(bf16[32,1280]{1,0:T(8,128)(2,1)} %get-tuple-element.507), channel_id=1, source_target_pairs={{4,0},{8,4},{12,8},{16,12},{20,16},{24,20},{28,24},{5,1},{9,5},{13... | collective-permute-start | bytes 245768 | tf_op jit(solution)/shard_map/while/body/eval_jaxpr/ppermute | solution.py:13
  176.6 70.2 %collective-permute-start = (bf16[32,2048]{1,0:T(8,128)(2,1)}, bf16[32,2048]{1,0:T(8,128)(2,1)S(1)}, u32[]{:S(2)}, u32[]{:S(2)}) collective-permute-start(bf16[32,2048]{1,0:T(8,128)(2,1)} %get-tuple-element.504), channel_id=1, source_target_pairs={{4,0},{8,4},{12,8},{16,12},{20,16},{24,20},{28,24},{5,1},{9,5},{13... | collective-permute-start | bytes 393224 | tf_op jit(solution)/shard_map/while/body/eval_jaxpr/ppermute | solution.py:13
  177.8 68.9 %collective-permute-start.1 = (bf16[32,1280]{1,0:T(8,128)(2,1)}, bf16[32,1280]{1,0:T(8,128)(2,1)S(1)}, u32[]{:S(2)}, u32[]{:S(2)}) collective-permute-start(bf16[32,1280]{1,0:T(8,128)(2,1)} %get-tuple-element.507), channel_id=1, source_target_pairs={{4,0},{8,4},{12,8},{16,12},{20,16},{24,20},{28,24},{5,1},{9,5},{13... | collective-permute-start | bytes 245768 | tf_op jit(solution)/shard_map/while/body/eval_jaxpr/ppermute | solution.py:13
  257.8 9.7 %collective-permute-start = (bf16[32,2048]{1,0:T(8,128)(2,1)}, bf16[32,2048]{1,0:T(8,128)(2,1)S(1)}, u32[]{:S(2)}, u32[]{:S(2)}) collective-permute-start(bf16[32,2048]{1,0:T(8,128)(2,1)} %get-tuple-element.504), channel_id=1, source_target_pairs={{4,0},{8,4},{12,8},{16,12},{20,16},{24,20},{28,24},{5,1},{9,5},{13... | collective-permute-start | bytes 393224 | tf_op jit(solution)/shard_map/while/body/eval_jaxpr/ppermute | solution.py:13
  259.1 8.4 %collective-permute-start.1 = (bf16[32,1280]{1,0:T(8,128)(2,1)}, bf16[32,1280]{1,0:T(8,128)(2,1)S(1)}, u32[]{:S(2)}, u32[]{:S(2)}) collective-permute-start(bf16[32,1280]{1,0:T(8,128)(2,1)} %get-tuple-element.507), channel_id=1, source_target_pairs={{4,0},{8,4},{12,8},{16,12},{20,16},{24,20},{28,24},{5,1},{9,5},{13... | collective-permute-start | bytes 245768 | tf_op jit(solution)/shard_map/while/body/eval_jaxpr/ppermute | solution.py:13
  267.4 6.9 %copy-start.2 = (f32[4,32,1280]{2,1,0:T(8,128)S(1)}, f32[4,32,1280]{2,1,0:T(8,128)}, u32[]{:S(2)}) copy-start(f32[4,32,1280]{2,1,0:T(8,128)} %get-tuple-element.319) | copy-start | bytes 1966084 | tf_op jit(solution)/shard_map/while/body/eval_jaxpr/cond
  278.5 9.1 %collective-permute-start = (bf16[32,2048]{1,0:T(8,128)(2,1)}, bf16[32,2048]{1,0:T(8,128)(2,1)S(1)}, u32[]{:S(2)}, u32[]{:S(2)}) collective-permute-start(bf16[32,2048]{1,0:T(8,128)(2,1)} %get-tuple-element.504), channel_id=1, source_target_pairs={{4,0},{8,4},{12,8},{16,12},{20,16},{24,20},{28,24},{5,1},{9,5},{13... | collective-permute-start | bytes 393224 | tf_op jit(solution)/shard_map/while/body/eval_jaxpr/ppermute | solution.py:13
  279.7 7.8 %collective-permute-start.1 = (bf16[32,1280]{1,0:T(8,128)(2,1)}, bf16[32,1280]{1,0:T(8,128)(2,1)S(1)}, u32[]{:S(2)}, u32[]{:S(2)}) collective-permute-start(bf16[32,1280]{1,0:T(8,128)(2,1)} %get-tuple-element.507), channel_id=1, source_target_pairs={{4,0},{8,4},{12,8},{16,12},{20,16},{24,20},{28,24},{5,1},{9,5},{13... | collective-permute-start | bytes 245768 | tf_op jit(solution)/shard_map/while/body/eval_jaxpr/ppermute | solution.py:13
  287.6 6.9 %copy-start.2 = (f32[4,32,1280]{2,1,0:T(8,128)S(1)}, f32[4,32,1280]{2,1,0:T(8,128)}, u32[]{:S(2)}) copy-start(f32[4,32,1280]{2,1,0:T(8,128)} %get-tuple-element.319) | copy-start | bytes 1966084 | tf_op jit(solution)/shard_map/while/body/eval_jaxpr/cond
  298.6 9.4 %collective-permute-start = (bf16[32,2048]{1,0:T(8,128)(2,1)}, bf16[32,2048]{1,0:T(8,128)(2,1)S(1)}, u32[]{:S(2)}, u32[]{:S(2)}) collective-permute-start(bf16[32,2048]{1,0:T(8,128)(2,1)} %get-tuple-element.504), channel_id=1, source_target_pairs={{4,0},{8,4},{12,8},{16,12},{20,16},{24,20},{28,24},{5,1},{9,5},{13... | collective-permute-start | bytes 393224 | tf_op jit(solution)/shard_map/while/body/eval_jaxpr/ppermute | solution.py:13
  299.9 8.1 %collective-permute-start.1 = (bf16[32,1280]{1,0:T(8,128)(2,1)}, bf16[32,1280]{1,0:T(8,128)(2,1)S(1)}, u32[]{:S(2)}, u32[]{:S(2)}) collective-permute-start(bf16[32,1280]{1,0:T(8,128)(2,1)} %get-tuple-element.507), channel_id=1, source_target_pairs={{4,0},{8,4},{12,8},{16,12},{20,16},{24,20},{28,24},{5,1},{9,5},{13... | collective-permute-start | bytes 245768 | tf_op jit(solution)/shard_map/while/body/eval_jaxpr/ppermute | solution.py:13
  319.0 8.5 %collective-permute-start = (bf16[32,2048]{1,0:T(8,128)(2,1)}, bf16[32,2048]{1,0:T(8,128)(2,1)S(1)}, u32[]{:S(2)}, u32[]{:S(2)}) collective-permute-start(bf16[32,2048]{1,0:T(8,128)(2,1)} %get-tuple-element.504), channel_id=1, source_target_pairs={{4,0},{8,4},{12,8},{16,12},{20,16},{24,20},{28,24},{5,1},{9,5},{13... | collective-permute-start | bytes 393224 | tf_op jit(solution)/shard_map/while/body/eval_jaxpr/ppermute | solution.py:13
  320.3 7.2 %collective-permute-start.1 = (bf16[32,1280]{1,0:T(8,128)(2,1)}, bf16[32,1280]{1,0:T(8,128)(2,1)S(1)}, u32[]{:S(2)}, u32[]{:S(2)}) collective-permute-start(bf16[32,1280]{1,0:T(8,128)(2,1)} %get-tuple-element.507), channel_id=1, source_target_pairs={{4,0},{8,4},{12,8},{16,12},{20,16},{24,20},{28,24},{5,1},{9,5},{13... | collective-permute-start | bytes 245768 | tf_op jit(solution)/shard_map/while/body/eval_jaxpr/ppermute | solution.py:13
  327.5 45.3 %all-gather.9.cloned.1.call-start = ((), (), s32[]{:S(2)}) async-start(), calls=%async_computation.3 | async-start | bytes 2621440 | tf_op jit(solution)/shard_map/all_gather | solution.py:90
  330.5 14.0 %all-to-all-start = ((bf16[4,128,320]{1,2,0:T(8,128)(2,1)}), bf16[4,128,320]{1,2,0:T(8,128)(2,1)S(1)}, u32[]{:S(2)}, u32[]{:S(2)}) async-start(bf16[4,128,320]{1,2,0:T(8,128)(2,1)} %copy.21), calls=%async_computation | async-start | bytes 655360 | tf_op jit(solution)/shard_map/all_to_all | solution.py:31
  344.5 13.0 %all-to-all-start.1 = ((bf16[4,128,512]{2,1,0:T(8,128)(2,1)}), bf16[4,128,512]{2,1,0:T(8,128)(2,1)}, u32[]{:S(2)}, u32[]{:S(2)}) async-start(bf16[4,128,512]{2,1,0:T(8,128)(2,1)} %copy.22), calls=%async_computation.1 | async-start | bytes 1048576 | tf_op jit(solution)/shard_map/all_to_all | solution.py:31
  (11 other events, 57.0 us)
Sparse Core Ops, SparseCore 0:
  9.5 31.9 all-gather.12
  43.1 58.2 all-gather.10
  327.6 20.3 all-gather.6
  349.4 23.2 all-gather.8

commit v2 on v1

v2 whole, which is shorter than its diff:
```python
import functools

import jax
import jax.numpy as jnp
from jax import lax
from jax.experimental import pallas as pl
from jax.experimental.pallas import tpu as pltpu
from jax.sharding import PartitionSpec as P

root_half = 0.7071067811865476
inv_root_tau = 0.3989422804014327
MESH = pl.DeviceIdType.MESH


def gelu_slope(preact):
    cumulative = 0.5 * (1.0 + lax.erf(preact * root_half))
    density = jnp.exp(-0.5 * preact * preact) * inv_root_tau
    return cumulative + preact * density


class Branch:
    def __init__(self, ins, outs, scratch):
        self.weight, self.saved, self.top = ins
        self.out, self.columns, self.local = outs
        (
            self.above,
            self.below,
            self.mine,
            self.pair_out,
            self.pair_in,
            self.chip_in,
            self.slope,
            self.saved_sem,
            self.top_sem,
            self.pair_sem,
            self.chip_sem,
            self.near_sem,
            self.far_sem,
            self.hop_sem,
            self.out_sem,
        ) = scratch


BRANCH_SCRATCH = 15


def kernel(sections, parts, micros, *refs):
    ins, outs, scratch = refs[:6], refs[6:12], refs[12:]
    branches = [
        Branch(ins[3 * b : 3 * b + 3], outs[3 * b : 3 * b + 3],
               scratch[BRANCH_SCRATCH * b : BRANCH_SCRATCH * (b + 1)])
        for b in range(2)
    ]
    section = lax.axis_index("section")
    me = lax.axis_index("dp")
    chips = parts // 2
    chip, core = me // 2, me % 2
    partner = chip * 2 + 1 - core
    is_last = section == sections - 1
    is_first = section == 0

    def ahead(k):
        return lax.rem(chip + k, chips) * 2 + core

    def behind(k):
        return lax.rem(chip + chips - k, chips) * 2 + core

    def other(group):
        return group + 1 - 2 * core

    def copy(src, dst, sems, index, where, part):
        return pltpu.make_async_remote_copy(
            src_ref=src, dst_ref=dst, send_sem=sems.at[(0, *index)], recv_sem=sems.at[(1, *index)],
            device_id=(where, part), device_id_type=MESH,
        )

    barrier = pltpu.get_barrier_semaphore()
    for k in range(1, parts):
        pl.semaphore_signal(barrier, inc=1, device_id=(section, lax.rem(me + k, parts)), device_id_type=MESH)

    @pl.when(section > 0)
    def _():
        pl.semaphore_signal(barrier, inc=1, device_id=(section - 1, me), device_id_type=MESH)

    @pl.when(section < sections - 1)
    def _():
        pl.semaphore_signal(barrier, inc=1, device_id=(section + 1, me), device_id_type=MESH)

    neighbours = lax.min(section, 1) + lax.min(sections - 1 - section, 1)
    pl.semaphore_wait(barrier, parts - 1 + neighbours)

    def saved_copy(br, m, k):
        to = lax.rem(me + k, parts)
        return copy(br.saved.at[to, m], br.columns.at[m, me], br.saved_sem, (m, k - 1), section, to)

    def top_copy(br, m, k):
        to = lax.rem(me + k, parts)
        return copy(br.top.at[to, m], br.above.at[m, me], br.top_sem, (m, k - 1), section, to)

    def pair_copy(br, m):
        return copy(br.pair_out.at[m], br.pair_in.at[m], br.pair_sem, (m,), section, partner)

    def chip_copy(br, m, k):
        return copy(br.mine.at[m, k], br.chip_in.at[m, k - 1], br.chip_sem, (m, k - 1), section, ahead(k))

    def near_copy(br, m, k):
        group = behind(k)
        return copy(br.local.at[m, group], br.local.at[m, group], br.near_sem, (m, k), section, partner)

    def far_copy(br, m, k):
        return copy(br.local.at[m, me], br.local.at[m, me], br.far_sem, (m, k - 1), section, ahead(k))

    def hop_copy(br, m):
        return copy(br.below.at[m], br.above.at[m], br.hop_sem, (m,), lax.max(section - 1, 0), me)

    def out_copy(br, m, k):
        to = lax.rem(me + k, parts)
        return copy(br.below.at[m, to], br.out.at[me, m], br.out_sem, (m, k - 1), section, to)

    def rows(block):
        return block.reshape(-1, block.shape[-1])

    def send_inputs(m):
        for br in branches:
            for k in range(1, parts):
                saved_copy(br, m, k).start()

            @pl.when(is_last)
            def _():
                for k in range(1, parts):
                    top_copy(br, m, k).start()

    def partial(m):
        for br in branches:
            br.columns[m, me] = br.saved[me, m]
            for k in range(1, parts):
                saved_copy(br, m, k).wait_recv()
            tokens = rows(br.columns[m])
            for k in range(chips):
                group = ahead(k)
                br.pair_out[m, k] = jnp.dot(
                    tokens, br.weight[other(group)], preferred_element_type=jnp.float32
                ).astype(jnp.bfloat16)
            pair_copy(br, m).start()
            for k in range(chips):
                br.mine[m, k] = jnp.dot(
                    tokens, br.weight[ahead(k)], preferred_element_type=jnp.float32
                ).astype(jnp.bfloat16)

    def pair_sum(m):
        for br in branches:
            pair_copy(br, m).wait_recv()
            for k in range(1, chips):
                both = br.mine[m, k].astype(jnp.float32) + br.pair_in[m, k].astype(jnp.float32)
                br.mine[m, k] = both.astype(jnp.bfloat16)
                chip_copy(br, m, k).start()

    def find_slope(m):
        for br in branches:
            total = br.mine[m, 0].astype(jnp.float32) + br.pair_in[m, 0].astype(jnp.float32)
            for k in range(1, chips):
                chip_copy(br, m, k).wait_recv()
                total = total + br.chip_in[m, k - 1].astype(jnp.float32)
            br.slope[m] = gelu_slope(total)

    def chain(m):
        for br in branches:
            @pl.when(is_last)
            def _():
                br.above[m, me] = br.top[me, m]
                for k in range(1, parts):
                    top_copy(br, m, k).wait_recv()

            @pl.when(jnp.logical_not(is_last))
            def _():
                hop_copy(br, m).wait_recv()

            br.local[m, me] = (rows(br.above[m]).astype(jnp.float32) * br.slope[m]).astype(jnp.bfloat16)
            for k in range(1, chips):
                far_copy(br, m, k).start()
            near_copy(br, m, 0).start()
        for br in branches:
            def through(group):
                return lax.dot_general(
                    br.local[m, group], br.weight[group], (((1,), (1,)), ((), ())),
                    preferred_element_type=jnp.float32,
                )

            total = rows(br.above[m]).astype(jnp.float32) + through(me)
            near_copy(br, m, 0).wait_recv()
            total = total + through(partner)
            for k in range(1, chips):
                far_copy(br, m, k).wait_recv()
                near_copy(br, m, k).start()
                total = total + through(behind(k))
            for k in range(1, chips):
                near_copy(br, m, k).wait_recv()
                total = total + through(other(behind(k)))
            br.below[m] = total.astype(jnp.bfloat16).reshape(br.below.shape[1:])

            @pl.when(jnp.logical_not(is_first))
            def _():
                hop_copy(br, m).start()

            br.out[me, m] = br.below[m, me]
            for k in range(1, parts):
                out_copy(br, m, k).start()

    def loop(body):
        pl.loop(0, micros)(body)

    loop(send_inputs)
    loop(partial)
    loop(pair_sum)

    @pl.loop(0, micros)
    def _(m):
        find_slope(m)
        chain(m)

    @pl.loop(0, micros)
    def _(m):
        for br in branches:
            for k in range(1, parts):
                saved_copy(br, m, k).wait_send()
                out_copy(br, m, k).wait_send()
                out_copy(br, m, k).wait_recv()

            @pl.when(is_last)
            def _():
                for k in range(1, parts):
                    top_copy(br, m, k).wait_send()

            @pl.when(jnp.logical_not(is_first))
            def _():
                hop_copy(br, m).wait_send()

            pair_copy(br, m).wait_send()
            near_copy(br, m, 0).wait_send()
            for k in range(1, chips):
                chip_copy(br, m, k).wait_send()
                far_copy(br, m, k).wait_send()
                near_copy(br, m, k).wait_send()


def branch_call(sections, weights, saveds, tops):
    operands, outs, scratch = [], [], []
    for weight, saved, top in zip(weights, saveds, tops):
        parts, rows, _ = weight.shape
        micros, tokens = saved.shape[1:3]
        chips = parts // 2
        everyone = parts * tokens
        operands += [weight, saved, top]
        outs += [
            jax.ShapeDtypeStruct((parts, micros, tokens, rows), jnp.bfloat16),
            jax.ShapeDtypeStruct((micros, parts, tokens, rows), jnp.bfloat16),
            jax.ShapeDtypeStruct((micros, parts, everyone, rows), jnp.bfloat16),
        ]
        dma = pltpu.SemaphoreType.DMA
        scratch += [
            pltpu.VMEM((micros, parts, tokens, rows), jnp.bfloat16),
            pltpu.VMEM((micros, parts, tokens, rows), jnp.bfloat16),
            pltpu.VMEM((micros, chips, everyone, rows), jnp.bfloat16),
            pltpu.VMEM((micros, chips, everyone, rows), jnp.bfloat16),
            pltpu.VMEM((micros, chips, everyone, rows), jnp.bfloat16),
            pltpu.VMEM((micros, max(chips - 1, 1), everyone, rows), jnp.bfloat16),
            pltpu.VMEM((micros, everyone, rows), jnp.float32),
            dma((2, micros, parts - 1)),
            dma((2, micros, parts - 1)),
            dma((2, micros)),
            dma((2, micros, max(chips - 1, 1))),
            dma((2, micros, chips)),
            dma((2, micros, max(chips - 1, 1))),
            dma((2, micros)),
            dma((2, micros, parts - 1)),
        ]
    vmem = pl.BlockSpec(memory_space=pltpu.VMEM)
    return pl.pallas_call(
        functools.partial(kernel, sections, parts, micros),
        out_shape=outs,
        in_specs=[vmem] * len(operands),
        out_specs=[vmem] * len(outs),
        scratch_shapes=scratch,
        compiler_params=pltpu.CompilerParams(
            collective_id=0, has_side_effects=True, vmem_limit_bytes=60 * 1024 * 1024
        ),
    )(*operands)


def feature_groups(block, parts):
    return jnp.moveaxis(block.reshape(*block.shape[:-1], parts, -1), -2, 0)


def weight_rows(columns, locals_all, scale):
    micros, parts, tokens, rows = columns.shape
    columns = columns.astype(jnp.bfloat16)
    by_group = locals_all.reshape(micros, parts, parts, tokens, rows)
    total = None
    for group in range(parts):
        left = columns[:, group].reshape(-1, rows)
        right = by_group[:, :, group].transpose(0, 2, 1, 3).reshape(micros * tokens, -1)
        term = lax.dot_general(
            left, right, (((0,), (0,)), ((), ())), preferred_element_type=jnp.float32
        )
        term = (term * scale).astype(jnp.bfloat16).astype(jnp.float32)
        total = term if total is None else total + term
    return total


def shards(vit_weight, t5_weight, vit_saved, t5_saved, vit_top_grad, t5_top_grad):
    sections = lax.axis_size("section")
    parts = lax.axis_size("dp")
    weights = [feature_groups(w[0], parts) for w in (t5_weight, vit_weight)]
    saveds = [feature_groups(s[0], parts) for s in (t5_saved, vit_saved)]
    tops = [feature_groups(t, parts) for t in (t5_top_grad, vit_top_grad)]
    micros, tokens = t5_top_grad.shape[:2]
    scale = 1.0 / (micros * tokens)
    results = branch_call(sections, weights, saveds, tops)
    grads, sums = [], []
    for b in range(2):
        out, columns, local = results[3 * b : 3 * b + 3]
        grads.append(jnp.moveaxis(out, 0, 2).reshape(micros, tokens, -1)[None])
        sums.append(weight_rows(columns, local, scale)[None])
    return (grads[1], grads[0], sums[1], sums[0])


def solution(mesh):
    placed = (
        P("section", "dp", None),
        P("section", "dp", None),
        P("section", None, "dp", None),
        P("section", None, "dp", None),
        P(None, "dp", None),
        P(None, "dp", None),
    )
    return jax.shard_map(
        shards,
        mesh=mesh,
        in_specs=placed,
        out_specs=(
            P("section", None, "dp", None),
            P("section", None, "dp", None),
            P("section", "dp", None),
            P("section", "dp", None),
        ),
        check_vma=False,
    )
```

time: 395 us -> 207 us (0.52)
  waiting for transfers between devices: 255 us -> 0 us
  Pallas kernels: 0 us -> 173 us
  matrix products: 58.6 us -> 8.3 us
  starting transfers between devices: 36.1 us -> 0 us
  between operations: 13.9 us -> 0.95 us
  other arithmetic: 9.35 us -> 0 us
    pallas_call x0 -> x1, Pallas kernels: none -> 173 us  [branch_call(): pl.pallas_call(functools.partial(kernel, sections, parts, micros), out_sh...]
    ppermute x22 -> x0, waiting for transfers between devices: 135 us -> none  [shifted(): return lax.ppermute(block, axis, route)]
    all_gather x4 -> x0, waiting for transfers between devices: 104 us -> none  [the longest x2 89.2 us: shards(): lax.all_gather(w[0], 'dp', axis=0, tiled=True)]
    dot_general x18 -> x8, matrix products: 58.6 us -> 8.3 us  [weight_rows(): lax.dot_general(left, right, (((0,), (0,)), ((), ())), preferred_element_...]
    ppermute x22 -> x0, starting transfers between devices: 28.3 us -> none  [shifted(): return lax.ppermute(block, axis, route)]
    all_to_all x2 -> x0, waiting for transfers between devices: 13.3 us -> none  [token_columns(): return lax.all_to_all(split, 'dp', 0, 0, tiled=True)]
    dynamic_update_slice x8 -> x0, other arithmetic: 9.35 us -> none  [advance(): lax.dynamic_update_index_in_dim(locals_now, local, slot, 0)]
    cond x30 -> x0, local copies, waits for them, and re-layouts: 8.99 us -> none
  transfers between devices with their start and end apart: 28 -> 0, of which waited for: 16 -> 0; matrix products, arithmetic and copies ran while one was open for 3% -> 0% of each run, Pallas kernels for 0% -> 0%
where the time goes in v2:
time: 207 us; the launch traced here: 206 us
  Pallas kernels  173 us (84%)
  local copies, waits for them, and re-layouts  24.5 us (12%)
  matrix products  8.3 us (4%)
    pallas_call x1, Pallas kernels, branch_call(): pl.pallas_call(functools.partial(kernel, sections, parts, micros), out_sh...  173 us
    dot_general x8, matrix products, weight_rows(): lax.dot_general(left, right, (((0,), (0,)), ((), ())), preferred_element_...  8.3 us
    another operation x6, local copies, waits for them, and re-layouts, feature_groups(): return jnp.moveaxis(block.reshape(*block.shape[:-1], parts, -1), -2, 0)  7.23 us
    unnamed x33, local copies, waits for them, and re-layouts  6.35 us

profile of v2, /device:TPU:0, one launch (start us, length us, event | category | flops | bytes accessed | tf_op | source)
XLA Modules:
  0.0 206.3 jit_solution(16614411691745957914)
XLA Ops:
  0.6 1.5 reshape_squeeze.39
  2.1 1.5 reshape.45
  3.6 1.1 copy_bitcast_fusion.6
  4.7 0.4 reshape_squeeze.37
  5.1 0.9 copy.51
  6.0 0.9 copy.50
  6.8 1.1 reshape_squeeze.38
  7.9 1.1 copy.49
  8.9 2.9 %copy.10 = bf16[1,512,2048]{1,2,0:T(8,128)(2,1)S(1)} copy(bf16[1,512,2048]{2,1,0:T(8,128)(2,1)} %param.7) | data formatting | bytes 4194304 | tf_op args[1]
  11.8 2.4 %copy.11 = bf16[512,4,512]{2,0,1:T(8,128)(2,1)} copy(bf16[512,4,512]{0,2,1:T(8,128)(2,1)S(1)} %bitcast.100) | data formatting | bytes 4194304 | tf_op jit(solution)/shard_map/reshape;squeeze | solution.py:291
  14.2 172.5 %shard_map.93 = (bf16[4,4,32,512]{3,2,1,0:T(8,128)(2,1)}, bf16[4,4,32,512]{3,2,1,0:T(8,128)(2,1)}, bf16[4,4,128,512]{3,2,1,0:T(8,128)(2,1)}, bf16[4,4,32,320]{3,...) custom-call(bf16[4,512,512]{2,1,0:T(8,128)(2,1)} %bitcast.99, ...), custom_call_target="tpu_custom_call" | custom-call | tf_op jit(solution)/shard_map/pallas_call | solution.py:278
  186.7 1.4 copy.17
  188.1 1.0 broadcast_in_dim_reshape.6
  189.2 1.6 copy.18
  190.7 1.2 broadcast_in_dim_reshape.7
  191.9 0.7 fusion.15
  193.1 0.3 reshape.47
  193.7 0.3 reshape.49
  194.2 0.3 reshape.48
  195.1 0.4 fusion.11
  195.5 0.4 fusion.7
  195.9 0.4 fusion.9
  196.4 1.6 fusion.5
  198.0 0.5 copy-done
  198.6 0.4 copy.31
  199.1 0.4 copy.33
  199.7 0.4 copy.32
  200.2 0.4 copy.34
  200.7 0.7 multiply_convert_fusion
  201.5 0.7 multiply_convert_fusion.2
  202.2 0.7 multiply_convert_fusion.1
  202.9 3.3 %add_bitcast_fusion = f32[1,512,2048]{2,1,0:T(8,128)} fusion(bf16[512,2048]{1,0:T(8,128)(2,1)S(1)} %multiply_convert_fusion, bf16[512,2048]{1,0:T(8,128)(2,1)S(1)} %multiply_convert_fusion.1, bf16[512,2048]{1,0:T(8,128)(2,1)S(1)} %multiply_convert_fusion.2, bf16[128,512]{1,0:T(8,128)(2,1)S(1)} %bitcast.118, bf16[128,2048]{1,0:T(8,128)(2,1)S(1)} %bitcast.102), kind=kOutput, calls=%fused_computation | convolution fusion | flops 277872640 | bytes 11141120 | tf_op jit(solution)/shard_map/dot_general | solution.py:302
  (31 shorter events, 2.0 us)
Async XLA Ops:
  0.6 4.0 %copy-start.3 = (bf16[1,4,32,2048]{3,2,1,0:T(8,128)(2,1)S(1)}, bf16[1,4,32,2048]{3,2,1,0:T(8,128)(2,1)}, u32[]{:S(2)}) copy-start(bf16[1,4,32,2048]{3,2,1,0:T(8,128)(2,1)} %param.9) | copy-start | bytes 1572868
  2.1 3.8 %copy-start.4 = (bf16[4,32,2048]{2,1,0:T(8,128)(2,1)S(1)}, bf16[4,32,2048]{2,1,0:T(8,128)(2,1)}, u32[]{:S(2)}) copy-start(bf16[4,32,2048]{2,1,0:T(8,128)(2,1)} %param.11) | copy-start | bytes 1572868
  3.6 3.2 %copy-start.2 = (bf16[1,320,1280]{2,1,0:T(8,128)(2,1)S(1)}, bf16[1,320,1280]{2,1,0:T(8,128)(2,1)}, u32[]{:S(2)}) copy-start(bf16[1,320,1280]{2,1,0:T(8,128)(2,1)} %param.6) | copy-start | bytes 2457604
  186.7 5.2 %copy-start.8 = (bf16[4,4,32,320]{3,2,1,0:T(8,128)(2,1)S(1)}, bf16[4,4,32,320]{3,2,1,0:T(8,128)(2,1)}, u32[]{:S(2)}) copy-start(bf16[4,4,32,320]{3,2,1,0:T(8,128)(2,1)} %get-tuple-element.12) | copy-start | bytes 983044
  186.7 5.9 %copy-start.5 = (bf16[4,4,32,512]{3,2,1,0:T(8,128)(2,1)S(1)}, bf16[4,4,32,512]{3,2,1,0:T(8,128)(2,1)}, u32[]{:S(2)}) copy-start(bf16[4,4,32,512]{3,2,1,0:T(8,128)(2,1)} %get-tuple-element.14) | copy-start | bytes 1572868
  189.2 3.5 %copy-start.1 = (bf16[4,4,128,320]{3,2,1,0:T(8,128)(2,1)S(1)}, bf16[4,4,128,320]{3,2,1,0:T(8,128)(2,1)}, u32[]{:S(2)}) copy-start(bf16[4,4,128,320]{3,2,1,0:T(8,128)(2,1)} %get-tuple-element.13) | copy-start | bytes 3932164
  193.4 1.6 copy-start.7
  194.2 1.3 copy-start.6
  195.5 0.9 copy-start.9
  196.4 2.1 %copy-start = (bf16[4,4,128,512]{3,2,1,0:T(8,128)(2,1)S(1)}, bf16[4,4,128,512]{3,2,1,0:T(8,128)(2,1)}, u32[]{:S(2)}) copy-start(bf16[4,4,128,512]{3,2,1,0:T(8,128)(2,1)} %get-tuple-element.15) | copy-start | bytes 6291460

commit v3 on v2

--- a/solution.py
+++ b/solution.py
@@ -120,32 +120,44 @@
     def rows(block):
         return block.reshape(-1, block.shape[-1])
 
-    def send_inputs(m):
+    def send_saved(m):
         for br in branches:
             for k in range(1, parts):
                 saved_copy(br, m, k).start()
 
-            @pl.when(is_last)
-            def _():
+    def send_top(m):
+        for br in branches:
+            for k in range(1, parts):
+                top_copy(br, m, k).start()
+
+    def partial(half):
+        size = micros // 2
+        first = half * size
+
+        @pl.loop(first, first + size)
+        def _(m):
+            for br in branches:
+                br.columns[m, me] = br.saved[me, m]
                 for k in range(1, parts):
-                    top_copy(br, m, k).start()
-
-    def partial(m):
-        for br in branches:
-            br.columns[m, me] = br.saved[me, m]
-            for k in range(1, parts):
-                saved_copy(br, m, k).wait_recv()
-            tokens = rows(br.columns[m])
+                    saved_copy(br, m, k).wait_recv()
+
+        span = pl.ds(first, size)
+        for br in branches:
+            tokens = rows(br.columns[span])
+
+            def product(group):
+                block = jnp.dot(tokens, br.weight[group], preferred_element_type=jnp.float32)
+                return block.astype(jnp.bfloat16).reshape(size, -1, block.shape[-1])
+
             for k in range(chips):
-                group = ahead(k)
-                br.pair_out[m, k] = jnp.dot(
-                    tokens, br.weight[other(group)], preferred_element_type=jnp.float32
-                ).astype(jnp.bfloat16)
-            pair_copy(br, m).start()
+                br.pair_out[span, k] = product(other(ahead(k)))
+
+            @pl.loop(first, first + size)
+            def _(m):
+                pair_copy(br, m).start()
+
             for k in range(chips):
-                br.mine[m, k] = jnp.dot(
-                    tokens, br.weight[ahead(k)], preferred_element_type=jnp.float32
-                ).astype(jnp.bfloat16)
+                br.mine[span, k] = product(ahead(k))
 
     def pair_sum(m):
         for br in branches:
@@ -155,18 +167,18 @@
                 br.mine[m, k] = both.astype(jnp.bfloat16)
                 chip_copy(br, m, k).start()
 
-    def find_slope(m):
-        for br in branches:
-            total = br.mine[m, 0].astype(jnp.float32) + br.pair_in[m, 0].astype(jnp.float32)
-            for k in range(1, chips):
-                chip_copy(br, m, k).wait_recv()
-                total = total + br.chip_in[m, k - 1].astype(jnp.float32)
-            br.slope[m] = gelu_slope(total)
-
-    def chain(m):
+    def find_slope(br, m):
+        total = br.mine[m, 0].astype(jnp.float32) + br.pair_in[m, 0].astype(jnp.float32)
+        for k in range(1, chips):
+            chip_copy(br, m, k).wait_recv()
+            total = total + br.chip_in[m, k - 1].astype(jnp.float32)
+        br.slope[m] = gelu_slope(total)
+
+    def spread(m):
         for br in branches:
             @pl.when(is_last)
             def _():
+                find_slope(br, m)
                 br.above[m, me] = br.top[me, m]
                 for k in range(1, parts):
                     top_copy(br, m, k).wait_recv()
@@ -179,6 +191,8 @@
             for k in range(1, chips):
                 far_copy(br, m, k).start()
             near_copy(br, m, 0).start()
+
+    def descend(m):
         for br in branches:
             def through(group):
                 return lax.dot_general(
@@ -186,12 +200,13 @@
                     preferred_element_type=jnp.float32,
                 )
 
+            for k in range(1, chips):
+                far_copy(br, m, k).wait_recv()
+                near_copy(br, m, k).start()
             total = rows(br.above[m]).astype(jnp.float32) + through(me)
             near_copy(br, m, 0).wait_recv()
             total = total + through(partner)
             for k in range(1, chips):
-                far_copy(br, m, k).wait_recv()
-                near_copy(br, m, k).start()
                 total = total + through(behind(k))
             for k in range(1, chips):
                 near_copy(br, m, k).wait_recv()
@@ -202,21 +217,56 @@
             def _():
                 hop_copy(br, m).start()
 
+    def hand_out(m):
+        for br in branches:
             br.out[me, m] = br.below[m, me]
             for k in range(1, parts):
                 out_copy(br, m, k).start()
 
-    def loop(body):
-        pl.loop(0, micros)(body)
-
-    loop(send_inputs)
-    loop(partial)
-    loop(pair_sum)
-
-    @pl.loop(0, micros)
-    def _(m):
-        find_slope(m)
-        chain(m)
+    ready = min(2, micros)
+    pl.loop(0, micros)(send_saved)
+
+    @pl.when(is_last)
+    def _():
+        pl.loop(0, ready)(send_top)
+
+    pl.loop(0, 2)(partial)
+
+    @pl.when(is_last)
+    def _():
+        pl.loop(0, ready)(pair_sum)
+
+    @pl.when(jnp.logical_not(is_last))
+    def _():
+        pl.loop(0, micros)(pair_sum)
+
+        @pl.loop(0, micros)
+        def _(m):
+            for br in branches:
+                find_slope(br, m)
+
+    @pl.loop(0, micros + 1)
+    def _(step):
+        @pl.when(step < micros)
+        def _():
+            spread(step)
+
+        @pl.when(jnp.logical_and(is_last, step < micros - ready))
+        def _():
+            pair_sum(step + ready)
+            send_top(step + ready)
+
+        @pl.when(step > 0)
+        def _():
+            descend(step - 1)
+
+        @pl.when(jnp.logical_and(section < 2, step > 0))
+        def _():
+            hand_out(step - 1)
+
+    @pl.when(section >= 2)
+    def _():
+        pl.loop(0, micros)(hand_out)
 
     @pl.loop(0, micros)
     def _(m):
@@ -311,10 +361,15 @@
     sections = lax.axis_size("section")
     parts = lax.axis_size("dp")
     weights = [feature_groups(w[0], parts) for w in (t5_weight, vit_weight)]
-    saveds = [feature_groups(s[0], parts) for s in (t5_saved, vit_saved)]
-    tops = [feature_groups(t, parts) for t in (t5_top_grad, vit_top_grad)]
     micros, tokens = t5_top_grad.shape[:2]
     scale = 1.0 / (micros * tokens)
+    cut = 2 if tokens % 32 == 0 else 1
+
+    def chunks(block):
+        return feature_groups(block.reshape(micros * cut, tokens // cut, -1), parts)
+
+    saveds = [chunks(s) for s in (t5_saved, vit_saved)]
+    tops = [chunks(t) for t in (t5_top_grad, vit_top_grad)]
     results = branch_call(sections, weights, saveds, tops)
     grads, sums = [], []
     for b in range(2):

time: 207 us -> 186 us (0.90)
  Pallas kernels: 173 us -> 152 us
    pallas_call x1, Pallas kernels: 173 us -> 152 us  [branch_call(): pl.pallas_call(functools.partial(kernel, sections, parts, micros), out_sh...]
    reshape x2 -> x0, local copies, waits for them, and re-layouts: 2.32 us -> none  [feature_groups(): return jnp.moveaxis(block.reshape(*block.shape[:-1], parts, -1), -2, 0)]
    another operation x6 -> x7, local copies, waits for them, and re-layouts: 7.23 us -> 8.15 us  [feature_groups(): return jnp.moveaxis(block.reshape(*block.shape[:-1], parts, -1), -2, 0)]
where the time goes in v3:
time: 186 us
  Pallas kernels  152 us (82%)
  local copies, waits for them, and re-layouts  24.2 us (13%)
  matrix products  8.3 us (4%)
    pallas_call x1, Pallas kernels, branch_call(): pl.pallas_call(functools.partial(kernel, sections, parts, micros), out_sh...  152 us
    dot_general x8, matrix products, weight_rows(): lax.dot_general(left, right, (((0,), (0,)), ((), ())), preferred_element_...  8.3 us
    another operation x7, local copies, waits for them, and re-layouts, feature_groups(): return jnp.moveaxis(block.reshape(*block.shape[:-1], parts, -1), -2, 0)  8.15 us
    unnamed x33, local copies, waits for them, and re-layouts  6.17 us

profile of v3, /device:TPU:0, one launch (start us, length us, event | category | flops | bytes accessed | tf_op | source)
XLA Modules:
  0.0 185.5 jit_solution(11916277993609870761)
XLA Ops:
  0.7 1.5 reshape_reshape.14
  2.2 1.4 reshape_reshape.15
  3.6 1.0 copy_bitcast_fusion.7
  4.6 0.4 reshape_reshape.12
  5.0 0.4 reshape_reshape.13
  5.4 1.2 copy_bitcast_fusion.1
  6.6 1.1 reshape_squeeze.31
  7.7 1.1 copy.48
  8.7 2.9 %copy.10 = bf16[1,512,2048]{1,2,0:T(8,128)(2,1)S(1)} copy(bf16[1,512,2048]{2,1,0:T(8,128)(2,1)} %param.7) | data formatting | bytes 4194304 | tf_op args[1]
  11.6 2.4 %copy.11 = bf16[512,4,512]{2,0,1:T(8,128)(2,1)} copy(bf16[512,4,512]{0,2,1:T(8,128)(2,1)S(1)} %bitcast.94) | data formatting | bytes 4194304 | tf_op jit(solution)/shard_map/reshape;squeeze | solution.py:341
  14.0 152.1 %shard_map.93 = (bf16[4,8,16,512]{3,2,1,0:T(8,128)(2,1)}, bf16[8,4,16,512]{3,2,1,0:T(8,128)(2,1)}, bf16[8,4,64,512]{3,2,1,0:T(8,128)(2,1)}, bf16[4,8,16,320]{3,2...) custom-call(bf16[4,512,512]{2,1,0:T(8,128)(2,1)} %bitcast.93, ...), custom_call_target="tpu_custom_call" | custom-call | tf_op jit(solution)/shard_map/pallas_call | solution.py:328
  166.1 1.4 copy.17
  167.4 1.0 broadcast_in_dim_reshape.6
  168.5 1.6 copy.18
  170.1 1.2 broadcast_in_dim_reshape.7
  171.2 0.7 fusion.15
  172.4 0.3 reshape.39
  172.9 0.3 reshape.41
  173.4 0.3 reshape.40
  174.2 0.4 fusion.11
  174.7 0.4 fusion.7
  175.1 0.4 fusion.9
  175.6 1.6 fusion.5
  177.1 0.5 copy-done
  177.9 0.4 copy.31
  178.4 0.4 copy.33
  178.9 0.4 copy.32
  179.5 0.4 copy.34
  180.0 0.7 multiply_convert_fusion
  180.7 0.7 multiply_convert_fusion.2
  181.5 0.7 multiply_convert_fusion.1
  182.2 3.3 %add_bitcast_fusion = f32[1,512,2048]{2,1,0:T(8,128)} fusion(bf16[512,2048]{1,0:T(8,128)(2,1)S(1)} %multiply_convert_fusion, bf16[512,2048]{1,0:T(8,128)(2,1)S(1)} %multiply_convert_fusion.1, bf16[512,2048]{1,0:T(8,128)(2,1)S(1)} %multiply_convert_fusion.2, bf16[128,512]{1,0:T(8,128)(2,1)S(1)} %bitcast.110, bf16[128,2048]{1,0:T(8,128)(2,1)S(1)} %bitcast.96), kind=kOutput, calls=%fused_computation | convolution fusion | flops 277872640 | bytes 11141120 | tf_op jit(solution)/shard_map/dot_general | solution.py:352
  (31 shorter events, 2.0 us)
Async XLA Ops:
  0.6 4.4 %copy-start.4 = (bf16[4,32,2048]{2,1,0:T(8,128)(2,1)S(1)}, bf16[4,32,2048]{2,1,0:T(8,128)(2,1)}, u32[]{:S(2)}) copy-start(bf16[4,32,2048]{2,1,0:T(8,128)(2,1)} %param.11) | copy-start | bytes 1572868
  0.6 4.0 %copy-start.3 = (bf16[1,4,32,2048]{3,2,1,0:T(8,128)(2,1)S(1)}, bf16[1,4,32,2048]{3,2,1,0:T(8,128)(2,1)}, u32[]{:S(2)}) copy-start(bf16[1,4,32,2048]{3,2,1,0:T(8,128)(2,1)} %param.9) | copy-start | bytes 1572868
  4.6 2.0 %copy-start.2 = (bf16[1,320,1280]{2,1,0:T(8,128)(2,1)S(1)}, bf16[1,320,1280]{2,1,0:T(8,128)(2,1)}, u32[]{:S(2)}) copy-start(bf16[1,320,1280]{2,1,0:T(8,128)(2,1)} %param.6) | copy-start | bytes 2457604
  166.0 5.2 %copy-start.8 = (bf16[8,4,16,320]{3,2,1,0:T(8,128)(2,1)S(1)}, bf16[8,4,16,320]{3,2,1,0:T(8,128)(2,1)}, u32[]{:S(2)}) copy-start(bf16[8,4,16,320]{3,2,1,0:T(8,128)(2,1)} %get-tuple-element.12) | copy-start | bytes 983044
  166.1 5.9 %copy-start.5 = (bf16[8,4,16,512]{3,2,1,0:T(8,128)(2,1)S(1)}, bf16[8,4,16,512]{3,2,1,0:T(8,128)(2,1)}, u32[]{:S(2)}) copy-start(bf16[8,4,16,512]{3,2,1,0:T(8,128)(2,1)} %get-tuple-element.14) | copy-start | bytes 1572868
  168.5 3.5 %copy-start.1 = (bf16[8,4,64,320]{3,2,1,0:T(8,128)(2,1)S(1)}, bf16[8,4,64,320]{3,2,1,0:T(8,128)(2,1)}, u32[]{:S(2)}) copy-start(bf16[8,4,64,320]{3,2,1,0:T(8,128)(2,1)} %get-tuple-element.13) | copy-start | bytes 3932164
  172.7 1.5 copy-start.7
  173.4 1.2 copy-start.6
  174.7 0.9 copy-start.9
  175.6 2.1 %copy-start = (bf16[8,4,64,512]{3,2,1,0:T(8,128)(2,1)S(1)}, bf16[8,4,64,512]{3,2,1,0:T(8,128)(2,1)}, u32[]{:S(2)}) copy-start(bf16[8,4,64,512]{3,2,1,0:T(8,128)(2,1)} %get-tuple-element.15) | copy-start | bytes 6291460

commit v4 on v3

--- a/solution.py
+++ b/solution.py
@@ -20,9 +20,12 @@
 
 class Branch:
     def __init__(self, ins, outs, scratch):
-        self.weight, self.saved, self.top = ins
+        self.weight_in, self.saved_in, self.top_in = ins
         self.out, self.columns, self.local = outs
         (
+            self.weight,
+            self.saved,
+            self.top,
             self.above,
             self.below,
             self.mine,
@@ -41,7 +44,7 @@
         ) = scratch
 
 
-BRANCH_SCRATCH = 15
+BRANCH_SCRATCH = 18
 
 
 def kernel(sections, parts, micros, *refs):
@@ -74,6 +77,11 @@
             device_id=(where, part), device_id_type=MESH,
         )
 
+    def regroup(source, groups):
+        size = groups.shape[-1]
+        for group in range(parts):
+            groups[group] = source[..., group * size : (group + 1) * size]
+
     barrier = pltpu.get_barrier_semaphore()
     for k in range(1, parts):
         pl.semaphore_signal(barrier, inc=1, device_id=(section, lax.rem(me + k, parts)), device_id_type=MESH)
@@ -86,6 +94,8 @@
     def _():
         pl.semaphore_signal(barrier, inc=1, device_id=(section + 1, me), device_id_type=MESH)
 
+    for br in branches:
+        regroup(br.saved_in, br.saved)
     neighbours = lax.min(section, 1) + lax.min(sections - 1 - section, 1)
     pl.semaphore_wait(barrier, parts - 1 + neighbours)
 
@@ -228,7 +238,12 @@
 
     @pl.when(is_last)
     def _():
+        for br in branches:
+            regroup(br.top_in, br.top)
         pl.loop(0, ready)(send_top)
+
+    for br in branches:
+        regroup(br.weight_in, br.weight)
 
     pl.loop(0, 2)(partial)
 
@@ -296,8 +311,9 @@
 def branch_call(sections, weights, saveds, tops):
     operands, outs, scratch = [], [], []
     for weight, saved, top in zip(weights, saveds, tops):
-        parts, rows, _ = weight.shape
-        micros, tokens = saved.shape[1:3]
+        rows, width = weight.shape
+        micros, tokens = saved.shape[:2]
+        parts = width // rows
         chips = parts // 2
         everyone = parts * tokens
         operands += [weight, saved, top]
@@ -308,6 +324,9 @@
         ]
         dma = pltpu.SemaphoreType.DMA
         scratch += [
+            pltpu.VMEM((parts, rows, rows), jnp.bfloat16),
+            pltpu.VMEM((parts, micros, tokens, rows), jnp.bfloat16),
+            pltpu.VMEM((parts, micros, tokens, rows), jnp.bfloat16),
             pltpu.VMEM((micros, parts, tokens, rows), jnp.bfloat16),
             pltpu.VMEM((micros, parts, tokens, rows), jnp.bfloat16),
             pltpu.VMEM((micros, chips, everyone, rows), jnp.bfloat16),
@@ -337,46 +356,83 @@
     )(*operands)
 
 
-def feature_groups(block, parts):
-    return jnp.moveaxis(block.reshape(*block.shape[:-1], parts, -1), -2, 0)
-
-
-def weight_rows(columns, locals_all, scale):
-    micros, parts, tokens, rows = columns.shape
-    columns = columns.astype(jnp.bfloat16)
-    by_group = locals_all.reshape(micros, parts, parts, tokens, rows)
-    total = None
-    for group in range(parts):
-        left = columns[:, group].reshape(-1, rows)
-        right = by_group[:, :, group].transpose(0, 2, 1, 3).reshape(micros * tokens, -1)
-        term = lax.dot_general(
-            left, right, (((0,), (0,)), ((), ())), preferred_element_type=jnp.float32
-        )
-        term = (term * scale).astype(jnp.bfloat16).astype(jnp.float32)
-        total = term if total is None else total + term
-    return total
+def finish_kernel(scale, *refs):
+    outs, buffers, sems = refs[6:10], refs[10:14], refs[14]
+    pending = []
+
+    def flush(src, dst):
+        copy = pltpu.make_async_copy(src, dst, sems.at[len(pending)])
+        copy.start()
+        pending.append(copy)
+
+    for b in (1, 0):
+        grads_in, columns, local = refs[3 * b : 3 * b + 3]
+        grads, sums = outs[2 * b : 2 * b + 2]
+        grad_buffer, sum_buffer = buffers[2 * b : 2 * b + 2]
+        micros, parts, tokens, rows = columns.shape
+        for part in range(parts):
+            grad_buffer[:, :, part * rows : (part + 1) * rows] = grads_in[part]
+        flush(grad_buffer, grads)
+        lefts = [columns[:, group].reshape(micros * tokens, rows) for group in range(parts)]
+        for part in range(parts):
+            span = pl.ds(part * rows, rows)
+            total = None
+            for group in range(parts):
+                right = local[:, part, group * tokens : (group + 1) * tokens]
+                term = lax.dot_general(
+                    lefts[group], right.reshape(micros * tokens, rows), (((0,), (0,)), ((), ())),
+                    preferred_element_type=jnp.float32,
+                )
+                term = (term * scale).astype(jnp.bfloat16).astype(jnp.float32)
+                total = term if total is None else total + term
+            sum_buffer[:, part * rows : (part + 1) * rows] = total
+            if rows % 128 == 0:
+                flush(sum_buffer.at[:, span], sums.at[:, span])
+        if rows % 128:
+            flush(sum_buffer, sums)
+    for copy in pending:
+        copy.wait()
+
+
+def finish(results, scale):
+    outs, buffers = [], []
+    for b in range(2):
+        parts, micros, tokens, rows = results[3 * b].shape
+        shapes = [((micros, tokens, parts * rows), jnp.bfloat16), ((rows, parts * rows), jnp.float32)]
+        outs += [jax.ShapeDtypeStruct(*shape) for shape in shapes]
+        buffers += [pltpu.VMEM(*shape) for shape in shapes]
+    return pl.pallas_call(
+        functools.partial(finish_kernel, scale),
+        out_shape=outs,
+        in_specs=[pl.BlockSpec(memory_space=pltpu.VMEM)] * 6,
+        out_specs=[pl.BlockSpec(memory_space=pl.ANY)] * 4,
+        scratch_shapes=buffers + [pltpu.SemaphoreType.DMA((2 * parts + 4,))],
+        compiler_params=pltpu.CompilerParams(vmem_limit_bytes=40 * 1024 * 1024),
+    )(*results)
 
 
 def shards(vit_weight, t5_weight, vit_saved, t5_saved, vit_top_grad, t5_top_grad):
     sections = lax.axis_size("section")
-    parts = lax.axis_size("dp")
-    weights = [feature_groups(w[0], parts) for w in (t5_weight, vit_weight)]
     micros, tokens = t5_top_grad.shape[:2]
     scale = 1.0 / (micros * tokens)
     cut = 2 if tokens % 32 == 0 else 1
 
     def chunks(block):
-        return feature_groups(block.reshape(micros * cut, tokens // cut, -1), parts)
-
-    saveds = [chunks(s) for s in (t5_saved, vit_saved)]
-    tops = [chunks(t) for t in (t5_top_grad, vit_top_grad)]
-    results = branch_call(sections, weights, saveds, tops)
-    grads, sums = [], []
-    for b in range(2):
-        out, columns, local = results[3 * b : 3 * b + 3]
-        grads.append(jnp.moveaxis(out, 0, 2).reshape(micros, tokens, -1)[None])
-        sums.append(weight_rows(columns, local, scale)[None])
-    return (grads[1], grads[0], sums[1], sums[0])
+        return block.reshape(micros * cut, tokens // cut, -1)
+
+    results = branch_call(
+        sections,
+        [t5_weight[0], vit_weight[0]],
+        [chunks(t5_saved[0]), chunks(vit_saved[0])],
+        [chunks(t5_top_grad), chunks(vit_top_grad)],
+    )
+    t5_grads, t5_sum, vit_grads, vit_sum = finish(results, scale)
+    return (
+        vit_grads.reshape(vit_saved.shape),
+        t5_grads.reshape(t5_saved.shape),
+        vit_sum[None],
+        t5_sum[None],
+    )
 
 
 def solution(mesh):

time: 186 us -> 165 us (0.89)
  local copies, waits for them, and re-layouts: 24.2 us -> 7.06 us
  matrix products: 8.3 us -> 0 us
  Pallas kernels: 152 us -> 157 us
    another operation x9 -> x0, local copies, waits for them, and re-layouts: 10.4 us -> none  [the longest x7 8.15 us: feature_groups(): return jnp.moveaxis(block.reshape(*block.shape[:-1], parts, -1), -2, 0)]
    dot_general x8 -> x0, matrix products: 8.3 us -> none  [weight_rows(): lax.dot_general(left, right, (((0,), (0,)), ((), ())), preferred_element_...]
    transpose x4 -> x0, local copies, waits for them, and re-layouts: 5.22 us -> none  [the longest x2 2.95 us: shards(): grads.append(jnp.moveaxis(out, 0, 2).reshape(micros, tokens, -1)[None])]
    pallas_call x0 -> x1, Pallas kernels: none -> 5.09 us  [finish(): pl.pallas_call(functools.partial(finish_kernel, scale), out_shape=outs, i...]
    unnamed x33 -> x12, local copies, waits for them, and re-layouts: 6.17 us -> 7.06 us
where the time goes in v4:
time: 165 us
  Pallas kernels  157 us (95%)
  local copies, waits for them, and re-layouts  7.06 us (4%)
    pallas_call x1, Pallas kernels, branch_call(): pl.pallas_call(functools.partial(kernel, sections, parts, micros), out_sh...  152 us
    unnamed x12, local copies, waits for them, and re-layouts  7.06 us
    pallas_call x1, Pallas kernels, finish(): pl.pallas_call(functools.partial(finish_kernel, scale), out_shape=outs, i...  5.09 us

profile of v4, /device:TPU:0, one launch (start us, length us, event | category | flops | bytes accessed | tf_op | source)
XLA Modules:
  0.0 164.8 jit_solution(10957202502898791618)
XLA Ops:
  0.6 152.0 %shard_map.93 = (bf16[4,8,16,512]{3,2,1,0:T(8,128)(2,1)}, bf16[8,4,16,512]{3,2,1,0:T(8,128)(2,1)}, bf16[8,4,64,512]{3,2,1,0:T(8,128)(2,1)}, bf16[4,8,16,320]{3,2...) custom-call(bf16[512,2048]{1,0:T(8,128)(2,1)} %bitcast.10, ...), custom_call_target="tpu_custom_call" | custom-call | tf_op jit(solution)/shard_map/pallas_call | solution.py:347
  152.6 0.0 copy-start
  152.6 1.6 copy-done
  154.2 0.0 copy-start.1
  154.2 1.4 copy-done.1
  155.6 0.0 copy-start.2
  155.6 1.0 copy-done.2
  156.6 0.0 copy-start.3
  156.7 1.0 copy-done.3
  157.7 0.0 copy-start.4
  157.7 1.0 copy-done.4
  158.7 0.0 copy-start.5
  158.7 1.0 copy-done.5
  159.7 5.1 %shard_map.94 = (bf16[8,16,2048]{2,1,0:T(8,128)(2,1)}, f32[512,2048]{1,0:T(8,128)}, bf16[8,16,1280]{2,1,0:T(8,128)(2,1)}, f32[320,1280]{1,0:T(8,128)}) custom-call(bf16[4,8,16,512]{3,2,1,0:T(8,128)(2,1)S(1)} %copy-done.2, bf16[8,4,16,512]{3,2,1,0:T(8,128)(2,1)S(1)} %copy-done.3, bf16[8,4,64,512]{3,2,1,0:T(8,128)(2,1)S(1)} %copy-done, ...), custom_call_target="tpu_custom_call" | custom-call | tf_op jit(solution)/shard_map/pallas_call | solution.py:404
Async XLA Ops:
  152.6 1.6 copy-start
  154.2 1.4 copy-start.1
  155.6 1.0 copy-start.2
  156.6 1.0 copy-start.3
  157.7 1.0 copy-start.4
  158.7 1.0 copy-start.5

commit v5 on v4

--- a/solution.py
+++ b/solution.py
@@ -27,6 +27,8 @@
             self.saved,
             self.top,
             self.above,
+            self.lifted,
+            self.lift_sem,
             self.below,
             self.mine,
             self.pair_out,
@@ -44,7 +46,7 @@
         ) = scratch
 
 
-BRANCH_SCRATCH = 18
+BRANCH_SCRATCH = 20
 
 
 def kernel(sections, parts, micros, *refs):
@@ -86,18 +88,30 @@
     for k in range(1, parts):
         pl.semaphore_signal(barrier, inc=1, device_id=(section, lax.rem(me + k, parts)), device_id_type=MESH)
 
-    @pl.when(section > 0)
+    def greet(other_section):
+        pl.semaphore_signal(barrier, inc=1, device_id=(other_section, me), device_id_type=MESH)
+
+    @pl.when(is_last)
     def _():
-        pl.semaphore_signal(barrier, inc=1, device_id=(section - 1, me), device_id_type=MESH)
-
-    @pl.when(section < sections - 1)
+        pl.loop(0, sections - 1)(greet)
+
+    @pl.when(jnp.logical_not(is_last))
     def _():
-        pl.semaphore_signal(barrier, inc=1, device_id=(section + 1, me), device_id_type=MESH)
+        greet(sections - 1)
+
+        @pl.when(section > 0)
+        def _():
+            greet(section - 1)
+
+        @pl.when(section < sections - 2)
+        def _():
+            greet(section + 1)
 
     for br in branches:
         regroup(br.saved_in, br.saved)
-    neighbours = lax.min(section, 1) + lax.min(sections - 1 - section, 1)
-    pl.semaphore_wait(barrier, parts - 1 + neighbours)
+    below_last = lax.min(sections - 1 - section, 1)
+    column = below_last * (1 + lax.min(section, 1) + lax.min(lax.max(sections - 2 - section, 0), 1))
+    pl.semaphore_wait(barrier, parts - 1 + column + (1 - below_last) * (sections - 1))
 
     def saved_copy(br, m, k):
         to = lax.rem(me + k, parts)
@@ -105,7 +119,13 @@
 
     def top_copy(br, m, k):
         to = lax.rem(me + k, parts)
-        return copy(br.top.at[to, m], br.above.at[m, me], br.top_sem, (m, k - 1), section, to)
+        return copy(br.top.at[to, m], br.lifted.at[m, me], br.top_sem, (m, k - 1), section, to)
+
+    def lift_copy(br, m):
+        return copy(br.lifted.at[m], br.above.at[m], br.lift_sem, (m,), sections - 1, me)
+
+    def helper(m):
+        return sections - 1 - lax.rem(m, sections)
 
     def pair_copy(br, m):
         return copy(br.pair_out.at[m], br.pair_in.at[m], br.pair_sem, (m,), section, partner)
@@ -184,14 +204,25 @@
             total = total + br.chip_in[m, k - 1].astype(jnp.float32)
         br.slope[m] = gelu_slope(total)
 
+    def gather_top(br, m):
+        br.lifted[m, me] = br.top[me, m]
+        for k in range(1, parts):
+            top_copy(br, m, k).wait_recv()
+
     def spread(m):
         for br in branches:
             @pl.when(is_last)
             def _():
                 find_slope(br, m)
-                br.above[m, me] = br.top[me, m]
-                for k in range(1, parts):
-                    top_copy(br, m, k).wait_recv()
+
+                @pl.when(helper(m) == section)
+                def _():
+                    gather_top(br, m)
+                    br.above[m] = br.lifted[m]
+
+                @pl.when(helper(m) != section)
+                def _():
+                    lift_copy(br, m).wait_recv()
 
             @pl.when(jnp.logical_not(is_last))
             def _():
@@ -236,11 +267,14 @@
     ready = min(2, micros)
     pl.loop(0, micros)(send_saved)
 
-    @pl.when(is_last)
-    def _():
-        for br in branches:
-            regroup(br.top_in, br.top)
-        pl.loop(0, ready)(send_top)
+    for br in branches:
+        regroup(br.top_in, br.top)
+
+    @pl.loop(0, micros)
+    def _(m):
+        @pl.when(helper(m) == section)
+        def _():
+            send_top(m)
 
     for br in branches:
         regroup(br.weight_in, br.weight)
@@ -253,6 +287,14 @@
 
     @pl.when(jnp.logical_not(is_last))
     def _():
+        @pl.loop(0, micros)
+        def _(m):
+            @pl.when(helper(m) == section)
+            def _():
+                for br in branches:
+                    gather_top(br, m)
+                    lift_copy(br, m).start()
+
         pl.loop(0, micros)(pair_sum)
 
         @pl.loop(0, micros)
@@ -269,7 +311,6 @@
         @pl.when(jnp.logical_and(is_last, step < micros - ready))
         def _():
             pair_sum(step + ready)
-            send_top(step + ready)
 
         @pl.when(step > 0)
         def _():
@@ -291,10 +332,14 @@
                 out_copy(br, m, k).wait_send()
                 out_copy(br, m, k).wait_recv()
 
-            @pl.when(is_last)
+            @pl.when(helper(m) == section)
             def _():
                 for k in range(1, parts):
                     top_copy(br, m, k).wait_send()
+
+                @pl.when(jnp.logical_not(is_last))
+                def _():
+                    lift_copy(br, m).wait_send()
 
             @pl.when(jnp.logical_not(is_first))
             def _():
@@ -328,6 +373,8 @@
             pltpu.VMEM((parts, micros, tokens, rows), jnp.bfloat16),
             pltpu.VMEM((parts, micros, tokens, rows), jnp.bfloat16),
             pltpu.VMEM((micros, parts, tokens, rows), jnp.bfloat16),
+            pltpu.VMEM((micros, parts, tokens, rows), jnp.bfloat16),
+            dma((2, micros)),
             pltpu.VMEM((micros, parts, tokens, rows), jnp.bfloat16),
             pltpu.VMEM((micros, chips, everyone, rows), jnp.bfloat16),
             pltpu.VMEM((micros, chips, everyone, rows), jnp.bfloat16),
@@ -358,6 +405,10 @@
 
 def finish_kernel(scale, *refs):
     outs, buffers, sems = refs[6:10], refs[10:14], refs[14]
+    staged, in_sems = refs[15:21], refs[21]
+    loads = [pltpu.make_async_copy(refs[i], staged[i], in_sems.at[i]) for i in range(6)]
+    for i in (3, 4, 5, 0, 1, 2):
+        loads[i].start()
     pending = []
 
     def flush(src, dst):
@@ -366,7 +417,9 @@
         pending.append(copy)
 
     for b in (1, 0):
-        grads_in, columns, local = refs[3 * b : 3 * b + 3]
+        grads_in, columns, local = staged[3 * b : 3 * b + 3]
+        for load in loads[3 * b : 3 * b + 3]:
+            load.wait()
         grads, sums = outs[2 * b : 2 * b + 2]
         grad_buffer, sum_buffer = buffers[2 * b : 2 * b + 2]
         micros, parts, tokens, rows = columns.shape
@@ -404,9 +457,12 @@
     return pl.pallas_call(
         functools.partial(finish_kernel, scale),
         out_shape=outs,
-        in_specs=[pl.BlockSpec(memory_space=pltpu.VMEM)] * 6,
+        in_specs=[pl.BlockSpec(memory_space=pl.ANY)] * 6,
         out_specs=[pl.BlockSpec(memory_space=pl.ANY)] * 4,
-        scratch_shapes=buffers + [pltpu.SemaphoreType.DMA((2 * parts + 4,))],
+        scratch_shapes=buffers
+        + [pltpu.SemaphoreType.DMA((2 * parts + 4,))]
+        + [pltpu.VMEM(result.shape, result.dtype) for result in results]
+        + [pltpu.SemaphoreType.DMA((6,))],
         compiler_params=pltpu.CompilerParams(vmem_limit_bytes=40 * 1024 * 1024),
     )(*results)
 

time: 165 us -> 159 us (0.964)
  Pallas kernels: 157 us -> 151 us
    pallas_call x1, Pallas kernels: 152 us -> 145 us  [branch_call(): pl.pallas_call(functools.partial(kernel, sections, parts, micros), out_sh...]
where the time goes in v5:
time: 159 us
  Pallas kernels  151 us (95%)
  local copies, waits for them, and re-layouts  7.06 us (4%)
    pallas_call x1, Pallas kernels, branch_call(): pl.pallas_call(functools.partial(kernel, sections, parts, micros), out_sh...  145 us
    unnamed x12, local copies, waits for them, and re-layouts  7.06 us
    pallas_call x1, Pallas kernels, finish(): pl.pallas_call(functools.partial(finish_kernel, scale), out_shape=outs, i...  5.67 us

profile of v5, /device:TPU:0, one launch (start us, length us, event | category | flops | bytes accessed | tf_op | source)
XLA Modules:
  0.0 158.6 jit_solution(6779934242084338917)
XLA Ops:
  0.6 145.2 %shard_map.93 = (bf16[4,8,16,512]{3,2,1,0:T(8,128)(2,1)}, bf16[8,4,16,512]{3,2,1,0:T(8,128)(2,1)}, bf16[8,4,64,512]{3,2,1,0:T(8,128)(2,1)}, bf16[4,8,16,320]{3,2...) custom-call(bf16[512,2048]{1,0:T(8,128)(2,1)} %bitcast.10, ...), custom_call_target="tpu_custom_call" | custom-call | tf_op jit(solution)/shard_map/pallas_call | solution.py:394
  145.9 0.0 copy-start
  145.9 1.6 copy-done
  147.5 0.0 copy-start.1
  147.5 1.4 copy-done.1
  148.9 0.0 copy-start.2
  148.9 1.0 copy-done.2
  149.9 0.0 copy-start.3
  149.9 1.0 copy-done.3
  151.0 0.0 copy-start.4
  151.0 1.0 copy-done.4
  152.0 0.0 copy-start.5
  152.0 1.0 copy-done.5
  153.0 5.7 %shard_map.94 = (bf16[8,16,2048]{2,1,0:T(8,128)(2,1)}, f32[512,2048]{1,0:T(8,128)}, bf16[8,16,1280]{2,1,0:T(8,128)(2,1)}, f32[320,1280]{1,0:T(8,128)}) custom-call(bf16[4,8,16,512]{3,2,1,0:T(8,128)(2,1)S(1)} %copy-done.2, bf16[8,4,16,512]{3,2,1,0:T(8,128)(2,1)S(1)} %copy-done.3, bf16[8,4,64,512]{3,2,1,0:T(8,128)(2,1)S(1)} %copy-done, ...), custom_call_target="tpu_custom_call" | custom-call | tf_op jit(solution)/shard_map/pallas_call | solution.py:457
Async XLA Ops:
  145.9 1.6 %copy-start = (bf16[8,4,64,512]{3,2,1,0:T(8,128)(2,1)S(1)}, bf16[8,4,64,512]{3,2,1,0:T(8,128)(2,1)}, u32[]{:S(2)}) copy-start(bf16[8,4,64,512]{3,2,1,0:T(8,128)(2,1)} %get-tuple-element.16.refs_2_) | copy-start | bytes 6291460
  147.5 1.4 copy-start.1
  148.9 1.0 copy-start.2
  149.9 1.0 copy-start.3
  151.0 1.0 copy-start.4
  152.0 1.0 copy-start.5

commit v6 on v5

--- a/solution.py
+++ b/solution.py
@@ -463,7 +463,7 @@
         + [pltpu.SemaphoreType.DMA((2 * parts + 4,))]
         + [pltpu.VMEM(result.shape, result.dtype) for result in results]
         + [pltpu.SemaphoreType.DMA((6,))],
-        compiler_params=pltpu.CompilerParams(vmem_limit_bytes=40 * 1024 * 1024),
+        compiler_params=pltpu.CompilerParams(vmem_limit_bytes=63 * 1024 * 1024),
     )(*results)
 
 

time: 159 us -> 153 us (0.962)
  local copies, waits for them, and re-layouts: 7.06 us -> 0 us
    unnamed x12 -> x0, local copies, waits for them, and re-layouts: 7.06 us -> none
where the time goes in v6:
time: 153 us
  Pallas kernels  152 us (99%)
    pallas_call x1, Pallas kernels, branch_call(): pl.pallas_call(functools.partial(kernel, sections, parts, micros), out_sh...  145 us
    pallas_call x1, Pallas kernels, finish(): pl.pallas_call(functools.partial(finish_kernel, scale), out_shape=outs, i...  6.64 us

profile of v6, /device:TPU:0, one launch (start us, length us, event | category | flops | bytes accessed | tf_op | source)
XLA Modules:
  0.0 152.5 jit_solution(179662997919391391)
XLA Ops:
  0.6 145.3 %shard_map.93 = (bf16[4,8,16,512]{3,2,1,0:T(8,128)(2,1)}, bf16[8,4,16,512]{3,2,1,0:T(8,128)(2,1)}, bf16[8,4,64,512]{3,2,1,0:T(8,128)(2,1)}, bf16[4,8,16,320]{3,2...) custom-call(bf16[512,2048]{1,0:T(8,128)(2,1)} %bitcast.10, ...), custom_call_target="tpu_custom_call" | custom-call | tf_op jit(solution)/shard_map/pallas_call | solution.py:394
  145.9 6.6 %shard_map.94 = (bf16[8,16,2048]{2,1,0:T(8,128)(2,1)}, f32[512,2048]{1,0:T(8,128)}, bf16[8,16,1280]{2,1,0:T(8,128)(2,1)}, f32[320,1280]{1,0:T(8,128)}) custom-call(bf16[4,8,16,512]{3,2,1,0:T(8,128)(2,1)} %get-tuple-element.14.refs_0_, bf16[8,4,16,512]{3,2,1,0:T(8,128)(2,1)} %get-tuple-element.15.refs_1_, bf16[8,4,64,512]{3,2,1,0:T(8,128)(2,1)} %get-tuple-element.16.refs_2_, ...), custom_call_target="tpu_custom_call" | custom-call | tf_op jit(solution)/shard_map/pallas_call | solution.py:457
